TPU v7x, 32 devices: a whole 2x2x4 slice. The times are simulated.
32 devices in a mesh: clip: 2 (over x), tm: 16 (over z, y, core).
Axes of the slice: x: 2, y: 2, z: 4, core: 2. Of those that a mesh axis runs over, the one named last changes fastest.
Arguments:
- frames: bfloat16 [64, 1024, 256], P('tm', 'clip'), parts along dimension 1, may hold values from -6 to 6
- gain_one: float32 [256], replicated, may hold values from 0.25 to 1.75
- conv_one: bfloat16 [3, 3, 3, 256, 256], replicated, may hold values from -0.078125 to 0.078125
- gain_two: float32 [256], replicated, may hold values from 0.25 to 1.75
- conv_two: bfloat16 [3, 3, 3, 256, 256], replicated, may hold values from -0.078125 to 0.078125
- out_weight: bfloat16 [256, 256], replicated, may hold values from -0.375 to 0.375
Outputs:
- latent: bfloat16 [64, 1024, 256], P(None, ('clip', 'tm')), parts along dimension 1
There are 2 independent parts, one for each index of `clip`. A program takes and returns all parts, laid end to end along the dimension named above; an argument that names none is the same for every part. Nothing has to cross between parts.
All inputs are finite; a program needn't handle non-finite values.
Results may differ from a plain program's by a relative error of at most 0.0065.
Values may be sent and summed in bfloat16 or wider, within the bound.
No kernel may reach another device: no remote copies, remote signals or barrier semaphores. Data moves between devices by JAX's collectives and lax.ppermute only.
A program may use at most 192 MiB of HBM per device.

v0:
```python
import jax
import jax.numpy as jnp
from jax import lax
from jax.sharding import PartitionSpec as P

ROWS = 4
COLS = 128


def passed_along(x, axis, by):
    size = lax.axis_size(axis)
    pairs = [(i, i + by) for i in range(size) if 0 <= i + by < size]
    return lax.ppermute(x, axis, pairs)


def norm_act(x, gain):
    values = x.astype(jnp.float32)
    scale = lax.rsqrt(jnp.mean(values * values, axis=-1, keepdims=True) + 1e-06)
    return jax.nn.silu(values * scale * gain).astype(jnp.bfloat16)


def causal_conv(act, kernel):
    extended = act.shape[0]
    outcount = extended - 2
    channels = act.shape[-1]
    grid = act.reshape(extended, ROWS, COLS, channels)
    padded = jnp.pad(grid, ((0, 0), (1, 1), (1, 1), (0, 0)))
    columns = jnp.concatenate(
        [
            padded[:, tap_r : tap_r + ROWS, tap_c : tap_c + COLS, :]
            for tap_r in range(3)
            for tap_c in range(3)
        ],
        axis=-1,
    )
    total = jnp.zeros((outcount * ROWS * COLS, channels), jnp.float32)
    for tap_t in range(3):
        window = columns[tap_t : tap_t + outcount].reshape(-1, 9 * channels)
        total = total + jnp.dot(
            window,
            kernel[tap_t].reshape(9 * channels, channels),
            preferred_element_type=jnp.float32,
        )
    return total.reshape(outcount, ROWS * COLS, channels)


def block_ext(extended, gain, kernel):
    act = norm_act(extended, gain)
    return (extended[2:].astype(jnp.float32) + causal_conv(act, kernel)).astype(jnp.bfloat16)


def with_previous(x):
    earlier = passed_along(x[-2:], "tm", 1)
    return jnp.concatenate([earlier, x], axis=0)


def body(frames, gain_one, conv_one, gain_two, conv_two, out_weight):
    channels = frames.shape[-1]
    local_frames = frames.shape[0]
    first = block_ext(with_previous(frames), gain_one, conv_one)
    source = with_previous(first)
    half = local_frames // 2
    received = []
    for index in range(2):
        part_out = block_ext(source[index * half : index * half + half + 2], gain_two, conv_two)
        result = jnp.dot(
            part_out.reshape(-1, channels), out_weight, preferred_element_type=jnp.float32
        )
        received.append(
            lax.all_to_all(
                result.reshape(part_out.shape).astype(jnp.bfloat16),
                "tm",
                split_axis=1,
                concat_axis=0,
                tiled=True,
            )
        )
    senders = received[0].shape[0] // half
    owned = received[0].shape[1]
    joined = jnp.concatenate(
        [piece.reshape(senders, half, owned, channels) for piece in received], axis=1
    )
    latent = joined.reshape(senders * local_frames, owned, channels)
    return latent


def solution(mesh):
    placed = (P("tm", "clip", None), P(), P(), P(), P(), P())
    return jax.shard_map(
        body, mesh=mesh, in_specs=placed, out_specs=P(None, ("clip", "tm"), None), check_vma=False
    )
```

profile of v0, /device:TPU:1, one launch (start us, length us, event | category | flops | bytes accessed | tf_op | source)
XLA Modules:
  0.0 102.4 jit_solution(9920365118946784368)
XLA Ops:
  0.0 1.1 %slice.138 = bf16[2,512,256]{2,1,0:T(8,128)(2,1)S(1)} slice(bf16[4,512,256]{2,1,0:T(8,128)(2,1)} %param.6), slice={[2:4], [0:512], [0:256]} | slice | bytes 1048576 | tf_op jit(solution)/shard_map/slice | solution.py:53
  1.1 4.7 %collective-permute-start = (bf16[2,512,256]{2,1,0:T(8,128)(2,1)S(1)}, bf16[2,512,256]{2,1,0:T(8,128)(2,1)S(1)}, u32[]{:S(2)}, u32[]{:S(2)}) collective-permute-start(bf16[2,512,256]{2,1,0:T(8,128)(2,1)S(1)} %slice.138), channel_id=1, source_target_pairs={{0,1},{1,2},{2,3},{3,4},{4,5},{5,6},{6,7},{7,8},{8,9},{9,10},{10,1... | collective-permute-start | bytes 1572872 | tf_op jit(solution)/shard_map/ppermute | solution.py:13
  5.8 3.7 %fusion.48 = (bf16[1,3,3,256,256]{4,3,2,1,0:T(8,128)(2,1)S(1)}, bf16[1,3,3,256,256]{4,3,2,1,0:T(8,128)(2,1)}, bf16[1,3,3,256,256]{4,3,2,1,0:T(8,128)(2,1)}) fusion(bf16[3,3,3,256,256]{4,3,2,1,0:T(8,128)(2,1)} %param.8), kind=kLoop, calls=%fused_computation.97 | loop fusion | bytes 7077888 | tf_op jit(solution)/shard_map/slice | solution.py:41
  9.5 2.4 %collective-permute-done = bf16[2,512,256]{2,1,0:T(8,128)(2,1)S(1)} collective-permute-done((bf16[2,512,256]{2,1,0:T(8,128)(2,1)S(1)}, bf16[2,512,256]{2,1,0:T(8,128)(2,1)S(1)}, u32[]{:S(2)}, u32[]{:S(2)}) %collective-permute-start) | collective-permute-done | bytes 524320 | tf_op jit(solution)/shard_map/ppermute | solution.py:13
  12.4 1.1 %multiply_convert_fusion = bf16[6,4,128,256]{3,2,1,0:T(8,128)(2,1)S(1)} fusion(bf16[4,4,128,256]{3,2,1,0:T(8,128)(2,1)S(1)} %bitcast.70, bf16[2,4,128,256]{3,2,1,0:T(8,128)(2,1)S(1)} %bitcast.81, f32[256]{0:T(256)S(1)} %copy-done.12, f32[6,4,128]{2,1,0:T(4,128)S(1)} %rsqrt.28), kind=kLoop, calls=%fused_computation.8 | loop fusion | flops 7077888 | bytes 3159040 | tf_op jit(solution)/shard_map/convert_element_type | solution.py:19
  14.1 0.6 fusion.18
  14.7 0.8 fusion.19
  15.6 0.8 fusion.20
  17.1 0.6 fusion.23
  17.7 7.6 %fusion.44 = (bf16[4,4,128,2304]{3,2,1,0:T(8,128)(2,1)S(1)}, bf16[4,4,128,2304]{3,2,1,0:T(8,128)(2,1)}, bf16[4,4,128,2304]{3,2,1,0:T(8,128)(2,1)}) fusion(bf16[6,4,128,2304]{3,2,1,0:T(8,128)(2,1)S(1)} %fusion.23), kind=kLoop, calls=%fused_computation.93 | loop fusion | bytes 56623104 | tf_op jit(solution)/shard_map/slice | solution.py:38
  25.3 5.3 %fusion.49 = f32[2048,256]{1,0:T(8,128)S(1)} fusion(bf16[2048,2304]{1,0:T(8,128)(2,1)} %bitcast.73, bf16[2304,256]{1,0:T(8,128)(2,1)S(1)} %bitcast.92), kind=kOutput, calls=%fused_computation.98 | convolution fusion | flops 2415919104 | bytes 12713984 | tf_op jit(solution)/shard_map/dot_general | solution.py:39
  30.6 1.1 %copy-done.2 = bf16[4,4,128,2304]{3,2,1,0:T(8,128)(2,1)S(1)} copy-done((bf16[4,4,128,2304]{3,2,1,0:T(8,128)(2,1)S(1)}, bf16[4,4,128,2304]{3,2,1,0:T(8,128)(2,1)}, u32[]{:S(2)}) %copy-start.2) | copy-done | bytes 9437208
  32.0 2.8 %convolution_add_fusion.1 = f32[2048,256]{1,0:T(8,128)S(1)} fusion(f32[2048,256]{1,0:T(8,128)S(1)} %fusion.49, bf16[2048,2304]{1,0:T(8,128)(2,1)S(1)} %bitcast.72, bf16[2304,256]{1,0:T(8,128)(2,1)S(1)} %bitcast.91), kind=kOutput, calls=%fused_computation.15 | convolution fusion | flops 2416443392 | bytes 14811136 | tf_op jit(solution)/shard_map/dot_general | solution.py:39
  34.8 2.8 %convolution_add_fusion = f32[2048,256]{1,0:T(8,128)S(1)} fusion(f32[2048,256]{1,0:T(8,128)S(1)} %convolution_add_fusion.1, bf16[2048,2304]{1,0:T(8,128)(2,1)S(1)} %bitcast.71, bf16[2304,256]{1,0:T(8,128)(2,1)S(1)} %bitcast.90), kind=kOutput, calls=%fused_computation.14 | convolution fusion | flops 2416443392 | bytes 14811136 | tf_op jit(solution)/shard_map/dot_general | solution.py:39
  38.0 4.7 %collective-permute-start.1 = (bf16[2,512,256]{2,1,0:T(8,128)(2,1)S(1)}, bf16[2,512,256]{2,1,0:T(8,128)(2,1)S(1)}, u32[]{:S(2)}, u32[]{:S(2)}) collective-permute-start(bf16[2,512,256]{2,1,0:T(8,128)(2,1)S(1)} %slice.185), channel_id=1, source_target_pairs={{0,1},{1,2},{2,3},{3,4},{4,5},{5,6},{6,7},{7,8},{8,9},{9,10},{10,1... | collective-permute-start | bytes 1572872 | tf_op jit(solution)/shard_map/ppermute | solution.py:13
  43.0 5.6 %collective-permute-done.1 = bf16[2,512,256]{2,1,0:T(8,128)(2,1)S(1)} collective-permute-done((bf16[2,512,256]{2,1,0:T(8,128)(2,1)S(1)}, bf16[2,512,256]{2,1,0:T(8,128)(2,1)S(1)}, u32[]{:S(2)}, u32[]{:S(2)}) %collective-permute-start.1) | collective-permute-done | bytes 524320 | tf_op jit(solution)/shard_map/ppermute | solution.py:13
  48.6 0.6 fusion
  49.3 1.4 %fusion.7 = (bf16[4,512,256]{2,1,0:T(8,128)(2,1)S(1)}, bf16[4,512,256]{2,1,0:T(8,128)(2,1)S(1)}) fusion(f32[256]{0:T(256)S(1)} %copy-done.13, f32[4,512]{1,0:T(4,128)S(1)} %get-tuple-element.25, bf16[4,512,256]{2,1,0:T(8,128)(2,1)S(1)} %add_convert_fusion, bf16[2,512,256]{2,1,0:T(8,128)(2,1)S(1)} %collective-permute-done.1, f32[4,512]{1,0:T(4,128)S(1)} %get-tuple-element.24), kind=kLoop, calls=%fused_computation.39 | loop fusion | flops 8912896 | bytes 3687424 | tf_op jit(solution)/shard_map/convert_element_type | solution.py:19
  52.6 1.4 %fusion.45 = (bf16[2,4,128,2304]{3,2,1,0:T(8,128)(2,1)S(1)}, bf16[2,4,128,2304]{3,2,1,0:T(8,128)(2,1)S(1)}, bf16[2,4,128,2304]{3,2,1,0:T(8,128)(2,1)S(1)}) fusion(bf16[4,4,128,2304]{3,2,1,0:T(8,128)(2,1)S(1)} %fusion.31), kind=kLoop, calls=%fused_computation.94 | loop fusion | bytes 28311552 | tf_op jit(solution)/shard_map/slice | solution.py:38
  54.0 1.4 %fusion.50 = f32[1024,256]{1,0:T(8,128)S(1)} fusion(bf16[1024,2304]{1,0:T(8,128)(2,1)S(1)} %bitcast.79, bf16[2304,256]{1,0:T(8,128)(2,1)S(1)} %bitcast.88), kind=kOutput, calls=%fused_computation.99 | convolution fusion | flops 1207959552 | bytes 6946816 | tf_op jit(solution)/shard_map/dot_general | solution.py:39
  55.4 1.4 %convolution_add_fusion.5 = f32[1024,256]{1,0:T(8,128)S(1)} fusion(f32[1024,256]{1,0:T(8,128)S(1)} %fusion.50, bf16[1024,2304]{1,0:T(8,128)(2,1)S(1)} %bitcast.77, bf16[2304,256]{1,0:T(8,128)(2,1)S(1)} %bitcast.86), kind=kOutput, calls=%fused_computation.60 | convolution fusion | flops 1208221696 | bytes 7995392 | tf_op jit(solution)/shard_map/dot_general | solution.py:39
  56.8 1.4 %convolution_add_fusion.4 = f32[1024,256]{1,0:T(8,128)S(1)} fusion(f32[1024,256]{1,0:T(8,128)S(1)} %convolution_add_fusion.5, bf16[1024,2304]{1,0:T(8,128)(2,1)S(1)} %bitcast.75, bf16[2304,256]{1,0:T(8,128)(2,1)S(1)} %bitcast.84), kind=kOutput, calls=%fused_computation.59 | convolution fusion | flops 1208221696 | bytes 7995392 | tf_op jit(solution)/shard_map/dot_general | solution.py:39
  58.6 1.3 %copy.8 = bf16[2,512,256]{2,0,1:T(2,128)(2,1)} copy(bf16[2,512,256]{2,1,0:T(8,128)(2,1)S(1)} %convolution_convert_fusion.1) | data formatting | bytes 1048576 | tf_op jit(solution)/shard_map/convert_element_type | solution.py:71
  59.9 8.0 %all-to-all-start = ((bf16[2,512,256]{2,0,1:T(2,128)(2,1)}), bf16[2,512,256]{2,0,1:T(2,128)(2,1)S(1)}, u32[]{:S(2)}, u32[]{:S(2)}) async-start(bf16[2,512,256]{2,0,1:T(2,128)(2,1)} %copy.8), calls=%async_computation | async-start | bytes 1048576 | tf_op jit(solution)/shard_map/all_to_all | solution.py:70
  69.8 1.4 %fusion.46 = (bf16[2,4,128,2304]{3,2,1,0:T(8,128)(2,1)S(1)}, bf16[2,4,128,2304]{3,2,1,0:T(8,128)(2,1)S(1)}, bf16[2,4,128,2304]{3,2,1,0:T(8,128)(2,1)S(1)}) fusion(bf16[4,4,128,2304]{3,2,1,0:T(8,128)(2,1)S(1)} %fusion.39), kind=kLoop, calls=%fused_computation.95 | loop fusion | bytes 28311552 | tf_op jit(solution)/shard_map/slice | solution.py:38
  71.3 1.4 %fusion.51 = f32[1024,256]{1,0:T(8,128)S(1)} fusion(bf16[1024,2304]{1,0:T(8,128)(2,1)S(1)} %bitcast.78, bf16[2304,256]{1,0:T(8,128)(2,1)S(1)} %bitcast.89), kind=kOutput, calls=%fused_computation.100 | convolution fusion | flops 1207959552 | bytes 6946816 | tf_op jit(solution)/shard_map/dot_general | solution.py:39
  72.7 1.4 %convolution_add_fusion.3 = f32[1024,256]{1,0:T(8,128)S(1)} fusion(f32[1024,256]{1,0:T(8,128)S(1)} %fusion.51, bf16[1024,2304]{1,0:T(8,128)(2,1)S(1)} %bitcast.76, bf16[2304,256]{1,0:T(8,128)(2,1)S(1)} %bitcast.87), kind=kOutput, calls=%fused_computation.58 | convolution fusion | flops 1208221696 | bytes 7995392 | tf_op jit(solution)/shard_map/dot_general | solution.py:39
  74.1 1.4 %convolution_add_fusion.2 = f32[1024,256]{1,0:T(8,128)S(1)} fusion(f32[1024,256]{1,0:T(8,128)S(1)} %convolution_add_fusion.3, bf16[1024,2304]{1,0:T(8,128)(2,1)S(1)} %bitcast.74, bf16[2304,256]{1,0:T(8,128)(2,1)S(1)} %bitcast.85), kind=kOutput, calls=%fused_computation.57 | convolution fusion | flops 1208221696 | bytes 7995392 | tf_op jit(solution)/shard_map/dot_general | solution.py:39
  76.3 5.6 %all-to-all-done = bf16[2,512,256]{2,0,1:T(2,128)(2,1)S(1)} async-done(((bf16[2,512,256]{2,0,1:T(2,128)(2,1)}), bf16[2,512,256]{2,0,1:T(2,128)(2,1)S(1)}, u32[]{:S(2)}, u32[]{:S(2)}) %all-to-all-start) | async-done | bytes 524320 | tf_op jit(solution)/shard_map/all_to_all | solution.py:70
  81.9 18.2 %all_to_all.30 = bf16[2,512,256]{2,0,1:T(2,128)(2,1)S(1)} all-to-all(bf16[2,512,256]{2,0,1:T(2,128)(2,1)S(1)} %copy.9), channel_id=1, replica_groups=mesh['clip'=2,'tm'=16] {'tm'}, dimensions={1} | all-to-all | bytes 1048576 | tf_op jit(solution)/shard_map/all_to_all | solution.py:70
  100.2 1.1 %pad_maximum_fusion.1 = bf16[16,4,32,256]{3,1,2,0:T(4,128)(2,1)S(1)} fusion(bf16[16,2,32,256]{3,1,2,0:T(2,128)(2,1)S(1)} %bitcast.83, bf16[16,2,32,256]{3,1,2,0:T(2,128)(2,1)S(1)} %bitcast.82), kind=kLoop, calls=%fused_computation.80 | loop fusion | flops 2097152 | bytes 2097152 | tf_op jit(solution)/shard_map/concatenate | solution.py:80
  101.2 1.2 %copy.10 = bf16[16,4,32,256]{3,2,1,0:T(8,128)(2,1)} copy(bf16[16,4,32,256]{3,1,2,0:T(4,128)(2,1)S(1)} %pad_maximum_fusion.1) | data formatting | bytes 2097152 | tf_op jit(solution)/shard_map/concatenate | solution.py:80
  (60 shorter events, 7.5 us)
Async XLA Ops:
  0.0 58.2 %copy-start = (bf16[256,256]{1,0:T(8,128)(2,1)S(1)}, bf16[256,256]{1,0:T(8,128)(2,1)}, u32[]{:S(2)}) copy-start(bf16[256,256]{1,0:T(8,128)(2,1)} %param.11) | copy-start | bytes 393220
  1.1 10.8 %copy-start.1 = (bf16[4,512,256]{2,1,0:T(8,128)(2,1)S(1)}, bf16[4,512,256]{2,1,0:T(8,128)(2,1)}, u32[]{:S(2)}) copy-start(bf16[4,512,256]{2,1,0:T(8,128)(2,1)} %param.6) | copy-start | bytes 3145732
  1.1 11.3 %copy-start.12 = (f32[256]{0:T(256)S(1)}, f32[256]{0:T(256)}, u32[]{:S(2)}) copy-start(f32[256]{0:T(256)} %param.7) | copy-start | bytes 3076
  1.1 10.8 %collective-permute-start = (bf16[2,512,256]{2,1,0:T(8,128)(2,1)S(1)}, bf16[2,512,256]{2,1,0:T(8,128)(2,1)S(1)}, u32[]{:S(2)}, u32[]{:S(2)}) collective-permute-start(bf16[2,512,256]{2,1,0:T(8,128)(2,1)S(1)} %slice.138), channel_id=1, source_target_pairs={{0,1},{1,2},{2,3},{3,4},{4,5},{5,6},{6,7},{7,8},{8,9},{9,10},{10,1... | collective-permute-start | bytes 1572872 | tf_op jit(solution)/shard_map/ppermute | solution.py:13
  17.6 7.6 %copy-start.11 = (bf16[1,3,3,256,256]{4,3,2,1,0:T(8,128)(2,1)S(1)}, bf16[1,3,3,256,256]{4,3,2,1,0:T(8,128)(2,1)}, u32[]{:S(2)}) copy-start(bf16[1,3,3,256,256]{4,3,2,1,0:T(8,128)(2,1)} %get-tuple-element.20) | copy-start | bytes 3538948
  25.3 6.4 %copy-start.2 = (bf16[4,4,128,2304]{3,2,1,0:T(8,128)(2,1)S(1)}, bf16[4,4,128,2304]{3,2,1,0:T(8,128)(2,1)}, u32[]{:S(2)}) copy-start(bf16[4,4,128,2304]{3,2,1,0:T(8,128)(2,1)} %get-tuple-element.8) | copy-start | bytes 28311556
  25.3 6.7 %copy-start.10 = (bf16[1,3,3,256,256]{4,3,2,1,0:T(8,128)(2,1)S(1)}, bf16[1,3,3,256,256]{4,3,2,1,0:T(8,128)(2,1)}, u32[]{:S(2)}) copy-start(bf16[1,3,3,256,256]{4,3,2,1,0:T(8,128)(2,1)} %get-tuple-element.21) | copy-start | bytes 3538948
  37.6 5.1 %copy-start.3 = (bf16[3,3,3,256,256]{4,3,2,1,0:T(8,128)(2,1)S(1)}, bf16[3,3,3,256,256]{4,3,2,1,0:T(8,128)(2,1)}, u32[]{:S(2)}) copy-start(bf16[3,3,3,256,256]{4,3,2,1,0:T(8,128)(2,1)} %param.10) | copy-start | bytes 10616836
  38.0 11.3 %copy-start.13 = (f32[256]{0:T(256)S(1)}, f32[256]{0:T(256)}, u32[]{:S(2)}) copy-start(f32[256]{0:T(256)} %param.9) | copy-start | bytes 3076
  38.0 10.6 %collective-permute-start.1 = (bf16[2,512,256]{2,1,0:T(8,128)(2,1)S(1)}, bf16[2,512,256]{2,1,0:T(8,128)(2,1)S(1)}, u32[]{:S(2)}, u32[]{:S(2)}) collective-permute-start(bf16[2,512,256]{2,1,0:T(8,128)(2,1)S(1)} %slice.185), channel_id=1, source_target_pairs={{0,1},{1,2},{2,3},{3,4},{4,5},{5,6},{6,7},{7,8},{8,9},{9,10},{10,1... | collective-permute-start | bytes 1572872 | tf_op jit(solution)/shard_map/ppermute | solution.py:13
  43.0 11.1 %copy-start.8 = (bf16[1,3,3,256,256]{4,3,2,1,0:T(8,128)(2,1)}, bf16[1,3,3,256,256]{4,3,2,1,0:T(8,128)(2,1)S(1)}, u32[]{:S(2)}) copy-start(bf16[1,3,3,256,256]{4,3,2,1,0:T(8,128)(2,1)S(1)} %get-tuple-element.17) | copy-start | bytes 3538948
  43.0 12.5 %copy-start.6 = (bf16[1,3,3,256,256]{4,3,2,1,0:T(8,128)(2,1)}, bf16[1,3,3,256,256]{4,3,2,1,0:T(8,128)(2,1)S(1)}, u32[]{:S(2)}) copy-start(bf16[1,3,3,256,256]{4,3,2,1,0:T(8,128)(2,1)S(1)} %get-tuple-element.18) | copy-start | bytes 3538948
  43.0 13.8 %copy-start.4 = (bf16[1,3,3,256,256]{4,3,2,1,0:T(8,128)(2,1)}, bf16[1,3,3,256,256]{4,3,2,1,0:T(8,128)(2,1)S(1)}, u32[]{:S(2)}) copy-start(bf16[1,3,3,256,256]{4,3,2,1,0:T(8,128)(2,1)S(1)} %get-tuple-element.16) | copy-start | bytes 3538948
  59.9 22.0 %all-to-all-start = ((bf16[2,512,256]{2,0,1:T(2,128)(2,1)}), bf16[2,512,256]{2,0,1:T(2,128)(2,1)S(1)}, u32[]{:S(2)}, u32[]{:S(2)}) async-start(bf16[2,512,256]{2,0,1:T(2,128)(2,1)} %copy.8), calls=%async_computation | async-start | bytes 1048576 | tf_op jit(solution)/shard_map/all_to_all | solution.py:70
  69.8 1.5 %copy-start.9 = (bf16[1,3,3,256,256]{4,3,2,1,0:T(8,128)(2,1)S(1)}, bf16[1,3,3,256,256]{4,3,2,1,0:T(8,128)(2,1)}, u32[]{:S(2)}) copy-start(bf16[1,3,3,256,256]{4,3,2,1,0:T(8,128)(2,1)} %copy-done.8) | copy-start | bytes 3538948
  71.3 1.4 %copy-start.7 = (bf16[1,3,3,256,256]{4,3,2,1,0:T(8,128)(2,1)S(1)}, bf16[1,3,3,256,256]{4,3,2,1,0:T(8,128)(2,1)}, u32[]{:S(2)}) copy-start(bf16[1,3,3,256,256]{4,3,2,1,0:T(8,128)(2,1)} %copy-done.6) | copy-start | bytes 3538948
  72.7 1.4 %copy-start.5 = (bf16[1,3,3,256,256]{4,3,2,1,0:T(8,128)(2,1)S(1)}, bf16[1,3,3,256,256]{4,3,2,1,0:T(8,128)(2,1)}, u32[]{:S(2)}) copy-start(bf16[1,3,3,256,256]{4,3,2,1,0:T(8,128)(2,1)} %copy-done.4) | copy-start | bytes 3538948
where the time goes:
time: 103 us; the launch traced here: 102 us
  local copies, waits for them, and re-layouts  27.7 us (27%)
  matrix products  19.8 us (19%)
  blocking collectives  18.2 us (18%)
  starting transfers between devices  17.4 us (17%)
  waiting for transfers between devices  13.6 us (13%)
  other arithmetic  5.04 us (5%)
    dot_general x9, matrix products, causal_conv(): jnp.dot(window, kernel[tap_t].reshape(9 * channels, channels), preferred_...  19.2 us
    all_to_all x1, blocking collectives, body(): lax.all_to_all(result.reshape(part_out.shape).astype(jnp.bfloat16), 'tm',...  18.2 us
    slice x3, local copies, waits for them, and re-layouts, causal_conv(): window = columns[tap_t:tap_t + outcount].reshape(-1, 9 * channels)  10.5 us
    ppermute x2, starting transfers between devices, passed_along(): return lax.ppermute(x, axis, pairs)  9.36 us
    unnamed x52, local copies, waits for them, and re-layouts  8.13 us
    ppermute x2, waiting for transfers between devices, passed_along(): return lax.ppermute(x, axis, pairs)  8.06 us
    all_to_all x1, starting transfers between devices, body(): lax.all_to_all(result.reshape(part_out.shape).astype(jnp.bfloat16), 'tm',...  8.04 us
    all_to_all x1, waiting for transfers between devices, body(): lax.all_to_all(result.reshape(part_out.shape).astype(jnp.bfloat16), 'tm',...  5.59 us
  transfers between devices with their start and end apart: 3, of which 3 were waited for; matrix products, arithmetic and copies ran while one was open for 12% of the time, Pallas kernels for 0%

commit v1 on v0

v1 whole, which is shorter than its diff:
```python
import functools

import jax
import jax.numpy as jnp
from jax import lax
from jax.experimental import pallas as pl
from jax.experimental.pallas import tpu as pltpu
from jax.sharding import PartitionSpec as P

ROWS = 4
COLS = 128
HALO = 2


def passed_along(x, axis, by):
    size = lax.axis_size(axis)
    pairs = [(i, i + by) for i in range(size) if 0 <= i + by < size]
    return lax.ppermute(x, axis, pairs)


def norm_act(x, gain):
    values = x.astype(jnp.float32)
    scale = lax.rsqrt(jnp.mean(values * values, axis=-1, keepdims=True) + 1e-06)
    gated = values * scale * gain
    return gated / (1.0 + jnp.exp(-gated))


def conv_body(groups, project, *refs):
    sources = refs[:groups]
    gain_ref, kernel_hbm = refs[groups], refs[groups + 1]
    rest = refs[groups + 2 :]
    if project:
        weight_ref, rest = rest[0], rest[1:]
    out_ref, taps_ref, sum_ref, kernel_ref, sems = rest
    channels = gain_ref.shape[-1]
    order = [(a, b) for b in (1, 0, 2) for a in range(3)]
    copies = {
        (a, b): pltpu.make_async_copy(kernel_hbm.at[a, b], kernel_ref.at[a, b], sems.at[a, b])
        for a, b in order
    }
    for key in order:
        copies[key].start()
    column = lax.broadcasted_iota(jnp.int32, (COLS, channels), 0)
    gain = gain_ref[...]

    for group, source in enumerate(sources):

        def prepare(i, carry, source=source, group=group):
            frame, row = i // ROWS, i % ROWS
            cells = pl.ds(pl.multiple_of(row * COLS, COLS), COLS)
            act = norm_act(source[frame, cells, :], gain)
            left = jnp.where(column == 0, 0.0, pltpu.roll(act, 1, 0))
            right = jnp.where(column == COLS - 1, 0.0, pltpu.roll(act, COLS - 1, 0))
            at = HALO * group + frame
            taps_ref[at, row, :, :channels] = left.astype(jnp.bfloat16)
            taps_ref[at, row, :, channels : 2 * channels] = act.astype(jnp.bfloat16)
            taps_ref[at, row, :, 2 * channels :] = right.astype(jnp.bfloat16)
            return carry

        lax.fori_loop(0, HALO * ROWS, prepare, 0, unroll=2)

    for part in range(groups - 1):
        base = HALO * part
        for a, b in order:
            if part == 0:
                copies[a, b].wait()
            first_in, first_out, count = {1: (0, 0, ROWS), 0: (0, 1, ROWS - 1), 2: (1, 0, ROWS - 1)}[b]
            window = taps_ref[base + a : base + a + HALO, first_in : first_in + count]
            product = jnp.dot(
                window.reshape(HALO * count * COLS, 3 * channels),
                kernel_ref[a, b],
                preferred_element_type=jnp.float32,
            ).reshape(HALO, count * COLS, channels)
            if (a, b) == order[0]:
                sum_ref[...] = product + sources[part + 1][...].astype(jnp.float32)
            else:
                sum_ref[:, first_out * COLS : (first_out + count) * COLS] += product
        block = sum_ref[...].astype(jnp.bfloat16)
        if project:
            block = jnp.dot(
                block.reshape(HALO * ROWS * COLS, channels),
                weight_ref[...],
                preferred_element_type=jnp.float32,
            ).astype(jnp.bfloat16)
            if len(out_ref.shape) == 4:
                owners, _, owned, _ = out_ref.shape
                block = block.reshape(HALO, owners, owned, channels)
                for frame in range(HALO):
                    out_ref[:, base + frame] = block[frame]
            else:
                out_ref[base : base + HALO] = block.reshape(HALO, ROWS * COLS, channels)
        else:
            out_ref[base : base + HALO] = block


def conv_block(sources, gain, kernel, weight=None, owners=None):
    groups = len(sources)
    outcount = HALO * (groups - 1)
    cells, channels = sources[0][0].shape[1:]
    flat_kernel = kernel.reshape(3, 3, 3 * channels, channels)
    whole = lambda *dims: pl.BlockSpec(dims, lambda i: (0,) * len(dims))
    operands = [array for array, _ in sources] + [gain.reshape(1, channels), flat_kernel]
    specs = [
        pl.BlockSpec((HALO, cells, channels), functools.partial(lambda at, i: (at, 0, 0), at))
        for _, at in sources
    ] + [whole(1, channels), pl.BlockSpec(memory_space=pl.ANY)]
    if weight is not None:
        operands.append(weight)
        specs.append(whole(channels, channels))
    if owners is not None:
        shape = (owners, outcount, cells // owners, channels)
    else:
        shape = (outcount, cells, channels)
    flops = 2 * outcount * cells * 27 * channels * channels
    return pl.pallas_call(
        functools.partial(conv_body, groups, weight is not None),
        grid=(1,),
        in_specs=specs,
        out_specs=whole(*shape),
        out_shape=jax.ShapeDtypeStruct(shape, jnp.bfloat16),
        scratch_shapes=[
            pltpu.VMEM((HALO * groups, ROWS, COLS, 3 * channels), jnp.bfloat16),
            pltpu.VMEM((HALO, cells, channels), jnp.float32),
            pltpu.VMEM((3, 3, 3 * channels, channels), jnp.bfloat16),
            pltpu.SemaphoreType.DMA((3, 3)),
        ],
        compiler_params=pltpu.CompilerParams(vmem_limit_bytes=56 * 1024 * 1024),
        cost_estimate=pl.CostEstimate(
            flops=flops, bytes_accessed=27 * channels * channels * 2, transcendentals=0
        ),
    )(*operands)


def body(frames, gain_one, conv_one, gain_two, conv_two, out_weight):
    local_frames, cells, channels = frames.shape
    members = lax.axis_size("tm")
    owned = cells // members
    assert local_frames == 2 * HALO
    earlier = passed_along(frames[-HALO:], "tm", 1)
    late = conv_block([(frames, 0), (frames, 1)], gain_one, conv_one)
    late_earlier = passed_along(late, "tm", 1)
    early = conv_block([(earlier, 0), (frames, 0)], gain_one, conv_one)
    aligned = owned % 16 == 0
    projected = conv_block(
        [(late_earlier, 0), (early, 0), (late, 0)],
        gain_two,
        conv_two,
        out_weight,
        members if aligned else None,
    )
    if aligned:
        latent = lax.all_to_all(projected, "tm", split_axis=0, concat_axis=0, tiled=True)
    else:
        latent = lax.all_to_all(projected, "tm", split_axis=1, concat_axis=0, tiled=True)
    return latent.reshape(members * local_frames, owned, channels)


def solution(mesh):
    placed = (P("tm", "clip", None), P(), P(), P(), P(), P())
    return jax.shard_map(
        body, mesh=mesh, in_specs=placed, out_specs=P(None, ("clip", "tm"), None), check_vma=False
    )
```

time: 103 us -> 81.1 us (0.79)
  Pallas kernels: 0 us -> 40 us
  local copies, waits for them, and re-layouts: 27.7 us -> 3.61 us
  matrix products: 19.8 us -> 0 us
  waiting for transfers between devices: 13.6 us -> 0.01 us
  blocking collectives: 18.2 us -> 30.6 us
  starting transfers between devices: 17.4 us -> 6.45 us
  other arithmetic: 5.04 us -> 0 us
    pallas_call x0 -> x3, Pallas kernels: none -> 40 us  [conv_block(): pl.pallas_call(functools.partial(conv_body, groups, weight is not None),...]
    dot_general x11 -> x0, matrix products: 19.8 us -> none  [the longest x9 19.2 us: causal_conv(): jnp.dot(window, kernel[tap_t].reshape(9 * channels, channels), preferred_...]
    slice x7 -> x1, local copies, waits for them, and re-layouts: 15.5 us -> 1.08 us  [body(): earlier = passed_along(frames[-HALO:], 'tm', 1)]
    all_to_all x1, blocking collectives: 18.2 us -> 30.6 us  [body(): lax.all_to_all(projected, 'tm', split_axis=0, concat_axis=0, tiled=True)]
    ppermute x2, waiting for transfers between devices: 8.06 us -> 0.01 us  [passed_along(): return lax.ppermute(x, axis, pairs)]
    all_to_all x1 -> x0, starting transfers between devices: 8.04 us -> none  [body(): lax.all_to_all(result.reshape(part_out.shape).astype(jnp.bfloat16), 'tm',...]
    unnamed x52 -> x5, local copies, waits for them, and re-layouts: 8.13 us -> 2.53 us
    all_to_all x1 -> x0, waiting for transfers between devices: 5.59 us -> none  [body(): lax.all_to_all(result.reshape(part_out.shape).astype(jnp.bfloat16), 'tm',...]
  transfers between devices with their start and end apart: 3 -> 2, of which waited for: 3 -> 0; matrix products, arithmetic and copies ran while one was open for 12% -> 0% of each run, Pallas kernels for 0% -> 27%
where the time goes in v1:
time: 81.1 us; the launch traced here: 80.8 us
  Pallas kernels  40 us (49%)
  blocking collectives  30.6 us (38%)
  starting transfers between devices  6.45 us (8%)
  local copies, waits for them, and re-layouts  3.61 us (4%)
    pallas_call x3, Pallas kernels, conv_block(): pl.pallas_call(functools.partial(conv_body, groups, weight is not None),...  40 us
    all_to_all x1, blocking collectives, body(): lax.all_to_all(projected, 'tm', split_axis=0, concat_axis=0, tiled=True)  30.6 us
    ppermute x2, starting transfers between devices, passed_along(): return lax.ppermute(x, axis, pairs)  6.45 us
    unnamed x5, local copies, waits for them, and re-layouts  2.53 us
  transfers between devices with their start and end apart: 2, of which 0 were waited for; matrix products, arithmetic and copies ran while one was open for 0% of the time, Pallas kernels for 27%

profile of v1, /device:TPU:1, one launch (start us, length us, event | category | flops | bytes accessed | tf_op | source)
XLA Modules:
  0.0 80.8 jit_solution(7019459918935066944)
XLA Ops:
  0.0 1.1 %slice.3 = bf16[2,512,256]{2,1,0:T(8,128)(2,1)S(1)} slice(bf16[4,512,256]{2,1,0:T(8,128)(2,1)} %refs_1_.3), slice={[2:4], [0:512], [0:256]} | slice | bytes 1048576 | tf_op jit(solution)/shard_map/slice | solution.py:139
  1.1 4.5 %collective-permute-start.1 = (bf16[2,512,256]{2,1,0:T(8,128)(2,1)S(1)}, bf16[2,512,256]{2,1,0:T(8,128)(2,1)S(1)}, u32[]{:S(2)}, u32[]{:S(2)}) collective-permute-start(bf16[2,512,256]{2,1,0:T(8,128)(2,1)S(1)} %slice.3), channel_id=1, source_target_pairs={{0,1},{1,2},{2,3},{3,4},{4,5},{5,6},{6,7},{7,8},{8,9},{9,10},{10,1... | collective-permute-start | bytes 1572872 | tf_op jit(solution)/shard_map/ppermute | solution.py:18
  5.6 10.8 %shard_map.64.refs_2_ = bf16[2,512,256]{2,1,0:T(8,128)(2,1)} custom-call(bf16[4,512,256]{2,1,0:T(8,128)(2,1)} %refs_1_.3, bf16[4,512,256]{2,1,0:T(8,128)(2,1)} %refs_1_.3, f32[1,256]{1,0:T(1,128)} %bitcast.9, bf16[3,3,768,256]{3,2,1,0:T(8,128)(2,1)} %bitcast.6), custom_call_target="tpu_custom_call" | custom-call | flops 3623878656 | bytes 3538944 | tf_op jit(solution)/shard_map/pallas_call | solution.py:115
  16.4 1.9 %collective-permute-start = (bf16[2,512,256]{2,1,0:T(8,128)(2,1)}, bf16[2,512,256]{2,1,0:T(8,128)(2,1)S(1)}, u32[]{:S(2)}, u32[]{:S(2)}) collective-permute-start(bf16[2,512,256]{2,1,0:T(8,128)(2,1)} %shard_map.64.refs_2_), channel_id=1, source_target_pairs={{0,1},{1,2},{2,3},{3,4},{4,5},{5,6},{6,7},{7,8},{8,9},{9,10},{10,1... | collective-permute-start | bytes 1572872 | tf_op jit(solution)/shard_map/ppermute | solution.py:18
  18.3 0.0 collective-permute-done.1.refs_0_
  18.3 0.0 copy-start.1
  18.3 0.8 copy-done.1
  19.1 10.8 %shard_map.65.refs_1_ = bf16[2,512,256]{2,1,0:T(8,128)(2,1)} custom-call(bf16[2,512,256]{2,1,0:T(8,128)(2,1)} %copy-done.1, bf16[4,512,256]{2,1,0:T(8,128)(2,1)} %refs_1_.3, f32[1,256]{1,0:T(1,128)} %bitcast.10, bf16[3,3,768,256]{3,2,1,0:T(8,128)(2,1)} %bitcast.7), custom_call_target="tpu_custom_call" | custom-call | flops 3623878656 | bytes 3538944 | tf_op jit(solution)/shard_map/pallas_call | solution.py:115
  29.9 0.0 collective-permute-done.refs_0_
  29.9 0.0 copy-start
  29.9 0.8 copy-done
  30.7 18.4 %shard_map.66 = bf16[16,4,32,256]{3,2,1,0:T(8,128)(2,1)} custom-call(bf16[2,512,256]{2,1,0:T(8,128)(2,1)} %copy-done, bf16[2,512,256]{2,1,0:T(8,128)(2,1)} %shard_map.65.refs_1_, bf16[2,512,256]{2,1,0:T(8,128)(2,1)} %shard_map.64.refs_2_, f32[1,256]{1,0:T(1,128)} %bitcast.11, bf16[3,3,768,256]{3,2,1,0:T(8,128)(2,1)} %bitcast.8, bf16[256,256]{1,0:T(8,128)(2,1)} %refs_5_.1), custom_call_target="tpu_custom_call" | custom-call | flops 7247757312 | bytes 3538944 | tf_op jit(solution)/shard_map/pallas_call | solution.py:115
  49.2 30.6 %all_to_all.5 = bf16[16,4,32,256]{3,2,1,0:T(8,128)(2,1)S(1)} all-to-all(bf16[16,4,32,256]{3,2,1,0:T(8,128)(2,1)} %shard_map.66), channel_id=1, replica_groups=mesh['clip'=2,'tm'=16] {'tm'}, dimensions={0} | all-to-all | bytes 2097152 | tf_op jit(solution)/shard_map/all_to_all | solution.py:152
  79.8 1.0 %copy.8 = bf16[64,32,256]{2,1,0:T(8,128)(2,1)} copy(bf16[64,32,256]{2,1,0:T(8,128)(2,1)S(1)} %bitcast.5) | data formatting | bytes 2097152
Async XLA Ops:
  1.1 17.2 %collective-permute-start.1 = (bf16[2,512,256]{2,1,0:T(8,128)(2,1)S(1)}, bf16[2,512,256]{2,1,0:T(8,128)(2,1)S(1)}, u32[]{:S(2)}, u32[]{:S(2)}) collective-permute-start(bf16[2,512,256]{2,1,0:T(8,128)(2,1)S(1)} %slice.3), channel_id=1, source_target_pairs={{0,1},{1,2},{2,3},{3,4},{4,5},{5,6},{6,7},{7,8},{8,9},{9,10},{10,1... | collective-permute-start | bytes 1572872 | tf_op jit(solution)/shard_map/ppermute | solution.py:18
  16.4 13.5 %collective-permute-start = (bf16[2,512,256]{2,1,0:T(8,128)(2,1)}, bf16[2,512,256]{2,1,0:T(8,128)(2,1)S(1)}, u32[]{:S(2)}, u32[]{:S(2)}) collective-permute-start(bf16[2,512,256]{2,1,0:T(8,128)(2,1)} %shard_map.64.refs_2_), channel_id=1, source_target_pairs={{0,1},{1,2},{2,3},{3,4},{4,5},{5,6},{6,7},{7,8},{8,9},{9,10},{10,1... | collective-permute-start | bytes 1572872 | tf_op jit(solution)/shard_map/ppermute | solution.py:18
  18.3 0.8 copy-start.1
  29.9 0.8 copy-start

commit v2 on v1

--- a/solution.py
+++ b/solution.py
@@ -10,6 +10,7 @@
 ROWS = 4
 COLS = 128
 HALO = 2
+VMEM_LIMIT = 24 * 1024 * 1024
 
 
 def passed_along(x, axis, by):
@@ -27,19 +28,12 @@
 
 def conv_body(groups, project, *refs):
     sources = refs[:groups]
-    gain_ref, kernel_hbm = refs[groups], refs[groups + 1]
+    gain_ref, kernel_ref = refs[groups], refs[groups + 1]
     rest = refs[groups + 2 :]
     if project:
         weight_ref, rest = rest[0], rest[1:]
-    out_ref, taps_ref, sum_ref, kernel_ref, sems = rest
+    out_ref, taps_ref, sum_ref = rest
     channels = gain_ref.shape[-1]
-    order = [(a, b) for b in (1, 0, 2) for a in range(3)]
-    copies = {
-        (a, b): pltpu.make_async_copy(kernel_hbm.at[a, b], kernel_ref.at[a, b], sems.at[a, b])
-        for a, b in order
-    }
-    for key in order:
-        copies[key].start()
     column = lax.broadcasted_iota(jnp.int32, (COLS, channels), 0)
     gain = gain_ref[...]
 
@@ -57,24 +51,17 @@
             taps_ref[at, row, :, 2 * channels :] = right.astype(jnp.bfloat16)
             return carry
 
-        lax.fori_loop(0, HALO * ROWS, prepare, 0, unroll=2)
+        lax.fori_loop(0, HALO * ROWS, prepare, 0, unroll=4)
 
     for part in range(groups - 1):
         base = HALO * part
-        for a, b in order:
-            if part == 0:
-                copies[a, b].wait()
-            first_in, first_out, count = {1: (0, 0, ROWS), 0: (0, 1, ROWS - 1), 2: (1, 0, ROWS - 1)}[b]
-            window = taps_ref[base + a : base + a + HALO, first_in : first_in + count]
-            product = jnp.dot(
-                window.reshape(HALO * count * COLS, 3 * channels),
-                kernel_ref[a, b],
-                preferred_element_type=jnp.float32,
-            ).reshape(HALO, count * COLS, channels)
-            if (a, b) == order[0]:
-                sum_ref[...] = product + sources[part + 1][...].astype(jnp.float32)
-            else:
-                sum_ref[:, first_out * COLS : (first_out + count) * COLS] += product
+        for row in range(ROWS):
+            bs = [b for b in range(3) if 0 <= row + b - 1 < ROWS]
+            kern = jnp.concatenate([kernel_ref[a, b] for b in bs for a in range(3)], axis=0)
+            win = jnp.concatenate([taps_ref[base + a : base + a + HALO, row + b - 1].reshape(HALO*COLS, 3*channels) for b in bs for a in range(3)], axis=1)
+            product = jnp.dot(win, kern, preferred_element_type=jnp.float32).reshape(HALO, COLS, channels)
+            at = slice(row * COLS, (row + 1) * COLS)
+            sum_ref[:, at] = product + sources[part + 1][:, at, :].astype(jnp.float32)
         block = sum_ref[...].astype(jnp.bfloat16)
         if project:
             block = jnp.dot(
@@ -103,7 +90,7 @@
     specs = [
         pl.BlockSpec((HALO, cells, channels), functools.partial(lambda at, i: (at, 0, 0), at))
         for _, at in sources
-    ] + [whole(1, channels), pl.BlockSpec(memory_space=pl.ANY)]
+    ] + [whole(1, channels), whole(3, 3, 3 * channels, channels)]
     if weight is not None:
         operands.append(weight)
         specs.append(whole(channels, channels))
@@ -121,10 +108,8 @@
         scratch_shapes=[
             pltpu.VMEM((HALO * groups, ROWS, COLS, 3 * channels), jnp.bfloat16),
             pltpu.VMEM((HALO, cells, channels), jnp.float32),
-            pltpu.VMEM((3, 3, 3 * channels, channels), jnp.bfloat16),
-            pltpu.SemaphoreType.DMA((3, 3)),
         ],
-        compiler_params=pltpu.CompilerParams(vmem_limit_bytes=56 * 1024 * 1024),
+        compiler_params=pltpu.CompilerParams(vmem_limit_bytes=VMEM_LIMIT),
         cost_estimate=pl.CostEstimate(
             flops=flops, bytes_accessed=27 * channels * channels * 2, transcendentals=0
         ),

time: 81.1 us -> 65.3 us (0.81)
  Pallas kernels: 40 us -> 18.7 us
  local copies, waits for them, and re-layouts: 3.61 us -> 5.96 us
  blocking collectives: 30.6 us -> 32.2 us
  waiting for transfers between devices: 0.01 us -> 1.13 us
    pallas_call x3, Pallas kernels: 40 us -> 18.7 us  [conv_block(): pl.pallas_call(functools.partial(conv_body, groups, weight is not None),...]
    unnamed x5 -> x13, local copies, waits for them, and re-layouts: 2.53 us -> 4.89 us
    all_to_all x1, blocking collectives: 30.6 us -> 32.2 us  [body(): lax.all_to_all(projected, 'tm', split_axis=0, concat_axis=0, tiled=True)]
    ppermute x2, waiting for transfers between devices: 0.01 us -> 1.13 us  [passed_along(): return lax.ppermute(x, axis, pairs)]
  transfers between devices with their start and end apart: 2 -> 2, of which waited for: 0 -> 1; matrix products, arithmetic and copies ran while one was open for 0% -> 0% of each run, Pallas kernels for 27% -> 15%
where the time goes in v2:
time: 65.3 us; the launch traced here: 65 us
  blocking collectives  32.2 us (49%)
  Pallas kernels  18.7 us (29%)
  starting transfers between devices  6.89 us (11%)
  local copies, waits for them, and re-layouts  5.96 us (9%)
  waiting for transfers between devices  1.13 us (2%)
    all_to_all x1, blocking collectives, body(): lax.all_to_all(projected, 'tm', split_axis=0, concat_axis=0, tiled=True)  32.2 us
    pallas_call x3, Pallas kernels, conv_block(): pl.pallas_call(functools.partial(conv_body, groups, weight is not None),...  18.7 us
    ppermute x2, starting transfers between devices, passed_along(): return lax.ppermute(x, axis, pairs)  6.89 us
    unnamed x13, local copies, waits for them, and re-layouts  4.89 us
  transfers between devices with their start and end apart: 2, of which 1 were waited for; matrix products, arithmetic and copies ran while one was open for 0% of the time, Pallas kernels for 15%

profile of v2, /device:TPU:1, one launch (start us, length us, event | category | flops | bytes accessed | tf_op | source)
XLA Modules:
  0.0 65.0 jit_solution(6740022985946545995)
XLA Ops:
  0.0 1.1 %slice.3 = bf16[2,512,256]{2,1,0:T(8,128)(2,1)S(1)} slice(bf16[4,512,256]{2,1,0:T(8,128)(2,1)} %refs_1_.3), slice={[2:4], [0:512], [0:256]} | slice | bytes 1048576 | tf_op jit(solution)/shard_map/slice | solution.py:124
  1.1 4.5 %collective-permute-start.1 = (bf16[2,512,256]{2,1,0:T(8,128)(2,1)S(1)}, bf16[2,512,256]{2,1,0:T(8,128)(2,1)S(1)}, u32[]{:S(2)}, u32[]{:S(2)}) collective-permute-start(bf16[2,512,256]{2,1,0:T(8,128)(2,1)S(1)} %slice.3), channel_id=1, source_target_pairs={{0,1},{1,2},{2,3},{3,4},{4,5},{5,6},{6,7},{7,8},{8,9},{9,10},{10,1... | collective-permute-start | bytes 1572872 | tf_op jit(solution)/shard_map/ppermute | solution.py:19
  5.6 0.0 copy-start
  5.6 1.2 %copy-done = bf16[4,512,256]{2,1,0:T(8,128)(2,1)S(1)} copy-done((bf16[4,512,256]{2,1,0:T(8,128)(2,1)S(1)}, bf16[4,512,256]{2,1,0:T(8,128)(2,1)}, u32[]{:S(2)}) %copy-start) | copy-done | bytes 1048600
  6.8 0.0 copy-start.1
  6.8 2.0 %copy-done.1 = bf16[3,3,3,256,256]{4,3,2,1,0:T(8,128)(2,1)S(1)} copy-done((bf16[3,3,3,256,256]{4,3,2,1,0:T(8,128)(2,1)S(1)}, bf16[3,3,3,256,256]{4,3,2,1,0:T(8,128)(2,1)}, u32[]{:S(2)}) %copy-start.1) | copy-done | bytes 3538968
  8.8 0.0 copy-start.4
  8.8 0.7 %copy-done.4 = f32[256]{0:T(256)S(1)} copy-done((f32[256]{0:T(256)S(1)}, f32[256]{0:T(256)}, u32[]{:S(2)}) %copy-start.4) | copy-done | bytes 1048
  9.5 4.8 %shard_map.64.refs_2_ = bf16[2,512,256]{2,1,0:T(8,128)(2,1)S(1)} custom-call(bf16[4,512,256]{2,1,0:T(8,128)(2,1)S(1)} %copy-done, bf16[4,512,256]{2,1,0:T(8,128)(2,1)S(1)} %copy-done, f32[1,256]{1,0:T(1,128)S(1)} %bitcast.8, bf16[3,3,768,256]{3,2,1,0:T(8,128)(2,1)S(1)} %bitcast.5), custom_call_target="tpu_custom_call" | custom-call | flops 3623878656 | bytes 3538944 | tf_op jit(solution)/shard_map/pallas_call | solution.py:102
  14.3 0.0 copy-start.2
  14.3 0.0 copy-start.3
  14.3 0.0 copy-start.5
  14.3 2.4 %collective-permute-start = (bf16[2,512,256]{2,1,0:T(8,128)(2,1)S(1)}, bf16[2,512,256]{2,1,0:T(8,128)(2,1)S(1)}, u32[]{:S(2)}, u32[]{:S(2)}) collective-permute-start(bf16[2,512,256]{2,1,0:T(8,128)(2,1)S(1)} %shard_map.64.refs_2_), channel_id=1, source_target_pairs={{0,1},{1,2},{2,3},{3,4},{4,5},{5,6},{6,7},{7,8},{8,9},{9,10},{10,1... | collective-permute-start | bytes 1572872 | tf_op jit(solution)/shard_map/ppermute | solution.py:19
  16.7 0.0 collective-permute-done.1.refs_0_
  16.7 4.8 %shard_map.65.refs_1_ = bf16[2,512,256]{2,1,0:T(8,128)(2,1)S(1)} custom-call(bf16[2,512,256]{2,1,0:T(8,128)(2,1)S(1)} %collective-permute-done.1.refs_0_, bf16[4,512,256]{2,1,0:T(8,128)(2,1)S(1)} %copy-done, f32[1,256]{1,0:T(1,128)S(1)} %bitcast.9, bf16[3,3,768,256]{3,2,1,0:T(8,128)(2,1)S(1)} %bitcast.6), custom_call_target="tpu_custom_call" | custom-call | flops 3623878656 | bytes 3538944 | tf_op jit(solution)/shard_map/pallas_call | solution.py:102
  21.5 1.1 %collective-permute-done.refs_0_ = bf16[2,512,256]{2,1,0:T(8,128)(2,1)S(1)} collective-permute-done((bf16[2,512,256]{2,1,0:T(8,128)(2,1)S(1)}, bf16[2,512,256]{2,1,0:T(8,128)(2,1)S(1)}, u32[]{:S(2)}, u32[]{:S(2)}) %collective-permute-start) | collective-permute-done | bytes 524320 | tf_op jit(solution)/shard_map/ppermute | solution.py:19
  22.6 0.0 copy-done.2
  22.6 0.0 copy-done.3
  22.6 0.0 copy-done.5
  22.6 9.1 %shard_map.66 = bf16[16,4,32,256]{3,2,1,0:T(8,128)(2,1)S(1)} custom-call(bf16[2,512,256]{2,1,0:T(8,128)(2,1)S(1)} %collective-permute-done.refs_0_, bf16[2,512,256]{2,1,0:T(8,128)(2,1)S(1)} %shard_map.65.refs_1_, bf16[2,512,256]{2,1,0:T(8,128)(2,1)S(1)} %shard_map.64.refs_2_, f32[1,256]{1,0:T(1,128)S(1)} %bitcast.10, bf16[3,3,768,256]{3,2,1,0:T(8,128)(2,1)S(1)} %bitcast.7, ...), custom_call_target="tpu_custom_call" | custom-call | flops 7247757312 | bytes 3538944 | tf_op jit(solution)/shard_map/pallas_call | solution.py:102
  31.8 32.2 %all_to_all.5 = bf16[16,4,32,256]{3,2,1,0:T(8,128)(2,1)S(1)} all-to-all(bf16[16,4,32,256]{3,2,1,0:T(8,128)(2,1)S(1)} %shard_map.66), channel_id=1, replica_groups=mesh['clip'=2,'tm'=16] {'tm'}, dimensions={0} | all-to-all | bytes 2097152 | tf_op jit(solution)/shard_map/all_to_all | solution.py:137
  64.0 1.0 %copy.8 = bf16[64,32,256]{2,1,0:T(8,128)(2,1)} copy(bf16[64,32,256]{2,1,0:T(8,128)(2,1)S(1)} %bitcast.11) | data formatting | bytes 2097152
Async XLA Ops:
  1.1 15.6 %collective-permute-start.1 = (bf16[2,512,256]{2,1,0:T(8,128)(2,1)S(1)}, bf16[2,512,256]{2,1,0:T(8,128)(2,1)S(1)}, u32[]{:S(2)}, u32[]{:S(2)}) collective-permute-start(bf16[2,512,256]{2,1,0:T(8,128)(2,1)S(1)} %slice.3), channel_id=1, source_target_pairs={{0,1},{1,2},{2,3},{3,4},{4,5},{5,6},{6,7},{7,8},{8,9},{9,10},{10,1... | collective-permute-start | bytes 1572872 | tf_op jit(solution)/shard_map/ppermute | solution.py:19
  5.6 1.2 %copy-start = (bf16[4,512,256]{2,1,0:T(8,128)(2,1)S(1)}, bf16[4,512,256]{2,1,0:T(8,128)(2,1)}, u32[]{:S(2)}) copy-start(bf16[4,512,256]{2,1,0:T(8,128)(2,1)} %refs_1_.3) | copy-start | bytes 3145732
  6.8 2.0 %copy-start.1 = (bf16[3,3,3,256,256]{4,3,2,1,0:T(8,128)(2,1)S(1)}, bf16[3,3,3,256,256]{4,3,2,1,0:T(8,128)(2,1)}, u32[]{:S(2)}) copy-start(bf16[3,3,3,256,256]{4,3,2,1,0:T(8,128)(2,1)} %param.8) | copy-start | bytes 10616836
  8.8 0.7 %copy-start.4 = (f32[256]{0:T(256)S(1)}, f32[256]{0:T(256)}, u32[]{:S(2)}) copy-start(f32[256]{0:T(256)} %param.7) | copy-start | bytes 3076
  14.3 8.3 %copy-start.2 = (bf16[3,3,3,256,256]{4,3,2,1,0:T(8,128)(2,1)S(1)}, bf16[3,3,3,256,256]{4,3,2,1,0:T(8,128)(2,1)}, u32[]{:S(2)}) copy-start(bf16[3,3,3,256,256]{4,3,2,1,0:T(8,128)(2,1)} %param.10) | copy-start | bytes 10616836
  14.3 8.3 %copy-start.3 = (bf16[256,256]{1,0:T(8,128)(2,1)S(1)}, bf16[256,256]{1,0:T(8,128)(2,1)}, u32[]{:S(2)}) copy-start(bf16[256,256]{1,0:T(8,128)(2,1)} %refs_5_.1) | copy-start | bytes 393220
  14.3 8.3 %copy-start.5 = (f32[256]{0:T(256)S(1)}, f32[256]{0:T(256)}, u32[]{:S(2)}) copy-start(f32[256]{0:T(256)} %param.9) | copy-start | bytes 3076
  14.3 8.3 %collective-permute-start = (bf16[2,512,256]{2,1,0:T(8,128)(2,1)S(1)}, bf16[2,512,256]{2,1,0:T(8,128)(2,1)S(1)}, u32[]{:S(2)}, u32[]{:S(2)}) collective-permute-start(bf16[2,512,256]{2,1,0:T(8,128)(2,1)S(1)} %shard_map.64.refs_2_), channel_id=1, source_target_pairs={{0,1},{1,2},{2,3},{3,4},{4,5},{5,6},{6,7},{7,8},{8,9},{9,10},{10,1... | collective-permute-start | bytes 1572872 | tf_op jit(solution)/shard_map/ppermute | solution.py:19

commit v3 on v2

--- a/solution.py
+++ b/solution.py
@@ -26,42 +26,92 @@
     return gated / (1.0 + jnp.exp(-gated))
 
 
-def conv_body(groups, project, *refs):
-    sources = refs[:groups]
-    gain_ref, kernel_ref = refs[groups], refs[groups + 1]
-    rest = refs[groups + 2 :]
+def spread(source, frame, row, gain, taps_ref, at):
+    channels = source.shape[-1]
+    column = lax.broadcasted_iota(jnp.int32, (COLS, channels), 0)
+    cells = pl.ds(pl.multiple_of(row * COLS, COLS), COLS)
+    act = norm_act(source[frame, cells, :], gain)
+    left = jnp.where(column == 0, 0.0, pltpu.roll(act, 1, 0))
+    right = jnp.where(column == COLS - 1, 0.0, pltpu.roll(act, COLS - 1, 0))
+    taps_ref[at, row, :, :channels] = left.astype(jnp.bfloat16)
+    taps_ref[at, row, :, channels : 2 * channels] = act.astype(jnp.bfloat16)
+    taps_ref[at, row, :, 2 * channels :] = right.astype(jnp.bfloat16)
+
+
+def taps_body(source, gain_ref, taps_ref):
+    gain = gain_ref[...]
+
+    def prepare(row, carry):
+        spread(source, 0, row, gain, taps_ref, 0)
+        return carry
+
+    lax.fori_loop(0, ROWS, prepare, 0, unroll=4)
+
+
+def taps_of(x, gain):
+    frames, cells, channels = x.shape
+    return pl.pallas_call(
+        taps_body,
+        grid=(frames,),
+        in_specs=[
+            pl.BlockSpec((1, cells, channels), lambda i: (i, 0, 0)),
+            pl.BlockSpec((1, channels), lambda i: (0, 0)),
+        ],
+        out_specs=pl.BlockSpec((1, ROWS, COLS, 3 * channels), lambda i: (i, 0, 0, 0)),
+        out_shape=jax.ShapeDtypeStruct((frames, ROWS, COLS, 3 * channels), jnp.bfloat16),
+        compiler_params=pltpu.CompilerParams(vmem_limit_bytes=VMEM_LIMIT),
+        cost_estimate=pl.CostEstimate(
+            flops=20 * frames * cells * channels, bytes_accessed=8 * frames * cells * channels, transcendentals=0
+        ),
+    )(x, gain.reshape(1, channels))
+
+
+def conv_body(ready, project, *refs):
+    groups = len(ready)
+    sources, refs = refs[:groups], list(refs[groups:])
+    residuals = [refs.pop(0) if ready[g] else sources[g] for g in range(1, groups)]
+    gain_ref, kernel_ref = refs[:2]
+    rest = refs[2:]
     if project:
         weight_ref, rest = rest[0], rest[1:]
     out_ref, taps_ref, sum_ref = rest
     channels = gain_ref.shape[-1]
-    column = lax.broadcasted_iota(jnp.int32, (COLS, channels), 0)
     gain = gain_ref[...]
 
     for group, source in enumerate(sources):
+        if ready[group]:
+            continue
 
         def prepare(i, carry, source=source, group=group):
             frame, row = i // ROWS, i % ROWS
-            cells = pl.ds(pl.multiple_of(row * COLS, COLS), COLS)
-            act = norm_act(source[frame, cells, :], gain)
-            left = jnp.where(column == 0, 0.0, pltpu.roll(act, 1, 0))
-            right = jnp.where(column == COLS - 1, 0.0, pltpu.roll(act, COLS - 1, 0))
-            at = HALO * group + frame
-            taps_ref[at, row, :, :channels] = left.astype(jnp.bfloat16)
-            taps_ref[at, row, :, channels : 2 * channels] = act.astype(jnp.bfloat16)
-            taps_ref[at, row, :, 2 * channels :] = right.astype(jnp.bfloat16)
+            spread(source, frame, row, gain, taps_ref, HALO * group + frame)
             return carry
 
         lax.fori_loop(0, HALO * ROWS, prepare, 0, unroll=4)
+
+    def tap(frame, row):
+        if ready[frame // HALO]:
+            return sources[frame // HALO][frame % HALO, row]
+        return taps_ref[frame, row]
 
     for part in range(groups - 1):
         base = HALO * part
         for row in range(ROWS):
-            bs = [b for b in range(3) if 0 <= row + b - 1 < ROWS]
-            kern = jnp.concatenate([kernel_ref[a, b] for b in bs for a in range(3)], axis=0)
-            win = jnp.concatenate([taps_ref[base + a : base + a + HALO, row + b - 1].reshape(HALO*COLS, 3*channels) for b in bs for a in range(3)], axis=1)
-            product = jnp.dot(win, kern, preferred_element_type=jnp.float32).reshape(HALO, COLS, channels)
+            taps = [(a, b) for b in range(3) if 0 <= row + b - 1 < ROWS for a in range(3)]
+            window = jnp.concatenate(
+                [
+                    jnp.concatenate([tap(base + a + f, row + b - 1) for f in range(HALO)], axis=0)
+                    for a, b in taps
+                ],
+                axis=1,
+            )
+            product = jnp.dot(
+                window,
+                jnp.concatenate([kernel_ref[a, b] for a, b in taps], axis=0),
+                preferred_element_type=jnp.float32,
+            ).reshape(HALO, COLS, channels)
             at = slice(row * COLS, (row + 1) * COLS)
-            sum_ref[:, at] = product + sources[part + 1][:, at, :].astype(jnp.float32)
+            sum_ref[:, at] = product + residuals[part][:, at, :].astype(jnp.float32)
         block = sum_ref[...].astype(jnp.bfloat16)
         if project:
             block = jnp.dot(
@@ -82,15 +132,23 @@
 
 def conv_block(sources, gain, kernel, weight=None, owners=None):
     groups = len(sources)
+    ready = tuple(len(source) == 3 for source in sources)
     outcount = HALO * (groups - 1)
     cells, channels = sources[0][0].shape[1:]
     flat_kernel = kernel.reshape(3, 3, 3 * channels, channels)
+    block_at = lambda at, *dims: pl.BlockSpec(dims, lambda i: (at,) + (0,) * (len(dims) - 1))
     whole = lambda *dims: pl.BlockSpec(dims, lambda i: (0,) * len(dims))
-    operands = [array for array, _ in sources] + [gain.reshape(1, channels), flat_kernel]
-    specs = [
-        pl.BlockSpec((HALO, cells, channels), functools.partial(lambda at, i: (at, 0, 0), at))
-        for _, at in sources
-    ] + [whole(1, channels), whole(3, 3, 3 * channels, channels)]
+    operands, specs = [], []
+    for source in sources:
+        array, dims = (source[2], (HALO, ROWS, COLS, 3 * channels)) if len(source) == 3 else (source[0], (HALO, cells, channels))
+        operands.append(array)
+        specs.append(block_at(source[1], *dims))
+    for source in sources[1:]:
+        if len(source) == 3:
+            operands.append(source[0])
+            specs.append(block_at(source[1], HALO, cells, channels))
+    operands += [gain.reshape(1, channels), flat_kernel]
+    specs += [whole(1, channels), whole(3, 3, 3 * channels, channels)]
     if weight is not None:
         operands.append(weight)
         specs.append(whole(channels, channels))
@@ -100,7 +158,7 @@
         shape = (outcount, cells, channels)
     flops = 2 * outcount * cells * 27 * channels * channels
     return pl.pallas_call(
-        functools.partial(conv_body, groups, weight is not None),
+        functools.partial(conv_body, ready, weight is not None),
         grid=(1,),
         in_specs=specs,
         out_specs=whole(*shape),
@@ -122,9 +180,10 @@
     owned = cells // members
     assert local_frames == 2 * HALO
     earlier = passed_along(frames[-HALO:], "tm", 1)
-    late = conv_block([(frames, 0), (frames, 1)], gain_one, conv_one)
+    taps = taps_of(frames, gain_one)
+    late = conv_block([(frames, 0, taps), (frames, 1, taps)], gain_one, conv_one)
     late_earlier = passed_along(late, "tm", 1)
-    early = conv_block([(earlier, 0), (frames, 0)], gain_one, conv_one)
+    early = conv_block([(earlier, 0), (frames, 0, taps)], gain_one, conv_one)
     aligned = owned % 16 == 0
     projected = conv_block(
         [(late_earlier, 0), (early, 0), (late, 0)],

time: 65.3 us -> 63.7 us (0.975)
  local copies, waits for them, and re-layouts: 5.96 us -> 4.43 us
  Pallas kernels: 18.7 us -> 17.8 us
  waiting for transfers between devices: 1.13 us -> 1.92 us
    unnamed x13, local copies, waits for them, and re-layouts: 4.89 us -> 3.35 us
    pallas_call x3 -> x4, Pallas kernels: 18.7 us -> 17.8 us  [the longest x3 16.3 us: conv_block(): pl.pallas_call(functools.partial(conv_body, ready, weight is not None), g...]
    ppermute x2, waiting for transfers between devices: 1.13 us -> 1.92 us  [passed_along(): return lax.ppermute(x, axis, pairs)]
  transfers between devices with their start and end apart: 2 -> 2, of which waited for: 1 -> 1; matrix products, arithmetic and copies ran while one was open for 0% -> 0% of each run, Pallas kernels for 15% -> 14%
where the time goes in v3:
time: 63.7 us; the launch traced here: 63.4 us
  blocking collectives  32.2 us (51%)
  Pallas kernels  17.8 us (28%)
  starting transfers between devices  6.89 us (11%)
  local copies, waits for them, and re-layouts  4.43 us (7%)
  waiting for transfers between devices  1.92 us (3%)
    all_to_all x1, blocking collectives, body(): lax.all_to_all(projected, 'tm', split_axis=0, concat_axis=0, tiled=True)  32.2 us
    pallas_call x3, Pallas kernels, conv_block(): pl.pallas_call(functools.partial(conv_body, ready, weight is not None), g...  16.3 us
    ppermute x2, starting transfers between devices, passed_along(): return lax.ppermute(x, axis, pairs)  6.89 us
    unnamed x13, local copies, waits for them, and re-layouts  3.35 us
    ppermute x2, waiting for transfers between devices, passed_along(): return lax.ppermute(x, axis, pairs)  1.92 us
    pallas_call x1, Pallas kernels, taps_of(): pl.pallas_call(taps_body, grid=(frames,), in_specs=[pl.BlockSpec((1, cell...  1.53 us
  transfers between devices with their start and end apart: 2, of which 1 were waited for; matrix products, arithmetic and copies ran while one was open for 0% of the time, Pallas kernels for 14%

profile of v3, /device:TPU:1, one launch (start us, length us, event | category | flops | bytes accessed | tf_op | source)
XLA Modules:
  0.0 63.4 jit_solution(2345851834976474168)
XLA Ops:
  0.0 1.1 %slice.3 = bf16[2,512,256]{2,1,0:T(8,128)(2,1)S(1)} slice(bf16[4,512,256]{2,1,0:T(8,128)(2,1)} %refs_2_.3), slice={[2:4], [0:512], [0:256]} | slice | bytes 1048576 | tf_op jit(solution)/shard_map/slice | solution.py:182
  1.1 4.5 %collective-permute-start.1 = (bf16[2,512,256]{2,1,0:T(8,128)(2,1)S(1)}, bf16[2,512,256]{2,1,0:T(8,128)(2,1)S(1)}, u32[]{:S(2)}, u32[]{:S(2)}) collective-permute-start(bf16[2,512,256]{2,1,0:T(8,128)(2,1)S(1)} %slice.3), channel_id=1, source_target_pairs={{0,1},{1,2},{2,3},{3,4},{4,5},{5,6},{6,7},{7,8},{8,9},{9,10},{10,1... | collective-permute-start | bytes 1572872 | tf_op jit(solution)/shard_map/ppermute | solution.py:19
  5.6 0.0 copy-start
  5.6 1.2 %copy-done = bf16[4,512,256]{2,1,0:T(8,128)(2,1)S(1)} copy-done((bf16[4,512,256]{2,1,0:T(8,128)(2,1)S(1)}, bf16[4,512,256]{2,1,0:T(8,128)(2,1)}, u32[]{:S(2)}) %copy-start) | copy-done | bytes 1048600
  6.8 0.0 copy-start.1
  6.8 0.7 %copy-done.1 = f32[256]{0:T(256)S(1)} copy-done((f32[256]{0:T(256)S(1)}, f32[256]{0:T(256)}, u32[]{:S(2)}) %copy-start.1) | copy-done | bytes 1048
  7.5 0.0 copy-start.2
  7.5 1.5 %shard_map.64.refs_0_.refs_1_ = bf16[4,4,128,768]{3,2,1,0:T(8,128)(2,1)S(1)} custom-call(bf16[4,512,256]{2,1,0:T(8,128)(2,1)S(1)} %copy-done, f32[1,256]{1,0:T(1,128)S(1)} %bitcast.5), custom_call_target="tpu_custom_call" | custom-call | flops 10485760 | bytes 4194304 | tf_op jit(solution)/shard_map/pallas_call | solution.py:53
  9.1 0.5 copy-done.2
  9.5 3.2 %shard_map.65.refs_2_ = bf16[2,512,256]{2,1,0:T(8,128)(2,1)S(1)} custom-call(bf16[4,4,128,768]{3,2,1,0:T(8,128)(2,1)S(1)} %shard_map.64.refs_0_.refs_1_, bf16[4,4,128,768]{3,2,1,0:T(8,128)(2,1)S(1)} %shard_map.64.refs_0_.refs_1_, bf16[4,512,256]{2,1,0:T(8,128)(2,1)S(1)} %copy-done, f32[1,256]{1,0:T(1,128)S(1)} %bitcast.6, bf16[3,3,768,256]{3,2,1,0:T(8,128)(2,1)S(1)} %bitcast.8), custom_call_target="tpu_custom_call" | custom-call | flops 3623878656 | bytes 3538944 | tf_op jit(solution)/shard_map/pallas_call | solution.py:160
  12.7 0.0 copy-start.3
  12.8 0.0 copy-start.4
  12.8 0.0 copy-start.5
  12.8 2.4 %collective-permute-start = (bf16[2,512,256]{2,1,0:T(8,128)(2,1)S(1)}, bf16[2,512,256]{2,1,0:T(8,128)(2,1)S(1)}, u32[]{:S(2)}, u32[]{:S(2)}) collective-permute-start(bf16[2,512,256]{2,1,0:T(8,128)(2,1)S(1)} %shard_map.65.refs_2_), channel_id=1, source_target_pairs={{0,1},{1,2},{2,3},{3,4},{4,5},{5,6},{6,7},{7,8},{8,9},{9,10},{10,1... | collective-permute-start | bytes 1572872 | tf_op jit(solution)/shard_map/ppermute | solution.py:19
  15.1 0.0 collective-permute-done.1.refs_0_
  15.2 4.0 %shard_map.66.refs_1_ = bf16[2,512,256]{2,1,0:T(8,128)(2,1)S(1)} custom-call(bf16[2,512,256]{2,1,0:T(8,128)(2,1)S(1)} %collective-permute-done.1.refs_0_, bf16[4,4,128,768]{3,2,1,0:T(8,128)(2,1)S(1)} %shard_map.64.refs_0_.refs_1_, bf16[4,512,256]{2,1,0:T(8,128)(2,1)S(1)} %copy-done, f32[1,256]{1,0:T(1,128)S(1)} %bitcast.7, bf16[3,3,768,256]{3,2,1,0:T(8,128)(2,1)S(1)} %bitcast.9), custom_call_target="tpu_custom_call" | custom-call | flops 3623878656 | bytes 3538944 | tf_op jit(solution)/shard_map/pallas_call | solution.py:160
  19.2 1.9 %collective-permute-done.refs_0_ = bf16[2,512,256]{2,1,0:T(8,128)(2,1)S(1)} collective-permute-done((bf16[2,512,256]{2,1,0:T(8,128)(2,1)S(1)}, bf16[2,512,256]{2,1,0:T(8,128)(2,1)S(1)}, u32[]{:S(2)}, u32[]{:S(2)}) %collective-permute-start) | collective-permute-done | bytes 524320 | tf_op jit(solution)/shard_map/ppermute | solution.py:19
  21.1 0.0 copy-done.3
  21.1 0.0 copy-done.4
  21.1 0.0 copy-done.5
  21.1 9.1 %shard_map.67 = bf16[16,4,32,256]{3,2,1,0:T(8,128)(2,1)S(1)} custom-call(bf16[2,512,256]{2,1,0:T(8,128)(2,1)S(1)} %collective-permute-done.refs_0_, bf16[2,512,256]{2,1,0:T(8,128)(2,1)S(1)} %shard_map.66.refs_1_, bf16[2,512,256]{2,1,0:T(8,128)(2,1)S(1)} %shard_map.65.refs_2_, f32[1,256]{1,0:T(1,128)S(1)} %bitcast.11, bf16[3,3,768,256]{3,2,1,0:T(8,128)(2,1)S(1)} %bitcast.10, ...), custom_call_target="tpu_custom_call" | custom-call | flops 7247757312 | bytes 3538944 | tf_op jit(solution)/shard_map/pallas_call | solution.py:160
  30.2 32.2 %all_to_all.5 = bf16[16,4,32,256]{3,2,1,0:T(8,128)(2,1)S(1)} all-to-all(bf16[16,4,32,256]{3,2,1,0:T(8,128)(2,1)S(1)} %shard_map.67), channel_id=1, replica_groups=mesh['clip'=2,'tm'=16] {'tm'}, dimensions={0} | all-to-all | bytes 2097152 | tf_op jit(solution)/shard_map/all_to_all | solution.py:196
  62.4 1.0 %copy.8 = bf16[64,32,256]{2,1,0:T(8,128)(2,1)} copy(bf16[64,32,256]{2,1,0:T(8,128)(2,1)S(1)} %bitcast.12) | data formatting | bytes 2097152
Async XLA Ops:
  1.1 14.1 %collective-permute-start.1 = (bf16[2,512,256]{2,1,0:T(8,128)(2,1)S(1)}, bf16[2,512,256]{2,1,0:T(8,128)(2,1)S(1)}, u32[]{:S(2)}, u32[]{:S(2)}) collective-permute-start(bf16[2,512,256]{2,1,0:T(8,128)(2,1)S(1)} %slice.3), channel_id=1, source_target_pairs={{0,1},{1,2},{2,3},{3,4},{4,5},{5,6},{6,7},{7,8},{8,9},{9,10},{10,1... | collective-permute-start | bytes 1572872 | tf_op jit(solution)/shard_map/ppermute | solution.py:19
  5.6 1.2 %copy-start = (bf16[4,512,256]{2,1,0:T(8,128)(2,1)S(1)}, bf16[4,512,256]{2,1,0:T(8,128)(2,1)}, u32[]{:S(2)}) copy-start(bf16[4,512,256]{2,1,0:T(8,128)(2,1)} %refs_2_.3) | copy-start | bytes 3145732
  6.8 0.7 %copy-start.1 = (f32[256]{0:T(256)S(1)}, f32[256]{0:T(256)}, u32[]{:S(2)}) copy-start(f32[256]{0:T(256)} %param.7) | copy-start | bytes 3076
  7.5 2.0 %copy-start.2 = (bf16[3,3,3,256,256]{4,3,2,1,0:T(8,128)(2,1)S(1)}, bf16[3,3,3,256,256]{4,3,2,1,0:T(8,128)(2,1)}, u32[]{:S(2)}) copy-start(bf16[3,3,3,256,256]{4,3,2,1,0:T(8,128)(2,1)} %param.8) | copy-start | bytes 10616836
  12.7 8.3 %copy-start.3 = (bf16[3,3,3,256,256]{4,3,2,1,0:T(8,128)(2,1)S(1)}, bf16[3,3,3,256,256]{4,3,2,1,0:T(8,128)(2,1)}, u32[]{:S(2)}) copy-start(bf16[3,3,3,256,256]{4,3,2,1,0:T(8,128)(2,1)} %param.10) | copy-start | bytes 10616836
  12.8 8.3 %copy-start.4 = (bf16[256,256]{1,0:T(8,128)(2,1)S(1)}, bf16[256,256]{1,0:T(8,128)(2,1)}, u32[]{:S(2)}) copy-start(bf16[256,256]{1,0:T(8,128)(2,1)} %refs_5_.1) | copy-start | bytes 393220
  12.8 8.3 %copy-start.5 = (f32[256]{0:T(256)S(1)}, f32[256]{0:T(256)}, u32[]{:S(2)}) copy-start(f32[256]{0:T(256)} %param.9) | copy-start | bytes 3076
  12.8 8.3 %collective-permute-start = (bf16[2,512,256]{2,1,0:T(8,128)(2,1)S(1)}, bf16[2,512,256]{2,1,0:T(8,128)(2,1)S(1)}, u32[]{:S(2)}, u32[]{:S(2)}) collective-permute-start(bf16[2,512,256]{2,1,0:T(8,128)(2,1)S(1)} %shard_map.65.refs_2_), channel_id=1, source_target_pairs={{0,1},{1,2},{2,3},{3,4},{4,5},{5,6},{6,7},{7,8},{8,9},{9,10},{10,1... | collective-permute-start | bytes 1572872 | tf_op jit(solution)/shard_map/ppermute | solution.py:19

commit v4 on v3

--- a/solution.py
+++ b/solution.py
@@ -29,7 +29,7 @@
 def spread(source, frame, row, gain, taps_ref, at):
     channels = source.shape[-1]
     column = lax.broadcasted_iota(jnp.int32, (COLS, channels), 0)
-    cells = pl.ds(pl.multiple_of(row * COLS, COLS), COLS)
+    cells = pl.ds(row * COLS, COLS)
     act = norm_act(source[frame, cells, :], gain)
     left = jnp.where(column == 0, 0.0, pltpu.roll(act, 1, 0))
     right = jnp.where(column == COLS - 1, 0.0, pltpu.roll(act, COLS - 1, 0))
@@ -41,11 +41,8 @@
 def taps_body(source, gain_ref, taps_ref):
     gain = gain_ref[...]
 
-    def prepare(row, carry):
+    for row in range(ROWS):
         spread(source, 0, row, gain, taps_ref, 0)
-        return carry
-
-    lax.fori_loop(0, ROWS, prepare, 0, unroll=4)
 
 
 def taps_of(x, gain):
@@ -82,12 +79,9 @@
         if ready[group]:
             continue
 
-        def prepare(i, carry, source=source, group=group):
-            frame, row = i // ROWS, i % ROWS
-            spread(source, frame, row, gain, taps_ref, HALO * group + frame)
-            return carry
-
-        lax.fori_loop(0, HALO * ROWS, prepare, 0, unroll=4)
+        for frame in range(HALO):
+            for row in range(ROWS):
+                spread(source, frame, row, gain, taps_ref, HALO * group + frame)
 
     def tap(frame, row):
         if ready[frame // HALO]:

time: 63.7 us -> 61.7 us (0.969)
  Pallas kernels: 17.8 us -> 15.3 us
  waiting for transfers between devices: 1.92 us -> 2.71 us
    pallas_call x3, Pallas kernels: 16.3 us -> 13.7 us  [conv_block(): pl.pallas_call(functools.partial(conv_body, ready, weight is not None), g...]
    ppermute x2, waiting for transfers between devices: 1.92 us -> 2.71 us  [passed_along(): return lax.ppermute(x, axis, pairs)]
  transfers between devices with their start and end apart: 2 -> 2, of which waited for: 1 -> 1; matrix products, arithmetic and copies ran while one was open for 0% -> 0% of each run, Pallas kernels for 14% -> 13%
where the time goes in v4:
time: 61.7 us; the launch traced here: 61.4 us
  blocking collectives  32.2 us (52%)
  Pallas kernels  15.3 us (25%)
  starting transfers between devices  6.71 us (11%)
  local copies, waits for them, and re-layouts  4.43 us (7%)
  waiting for transfers between devices  2.71 us (4%)
    all_to_all x1, blocking collectives, body(): lax.all_to_all(projected, 'tm', split_axis=0, concat_axis=0, tiled=True)  32.2 us
    pallas_call x3, Pallas kernels, conv_block(): pl.pallas_call(functools.partial(conv_body, ready, weight is not None), g...  13.7 us
    ppermute x2, starting transfers between devices, passed_along(): return lax.ppermute(x, axis, pairs)  6.71 us
    unnamed x13, local copies, waits for them, and re-layouts  3.35 us
    ppermute x2, waiting for transfers between devices, passed_along(): return lax.ppermute(x, axis, pairs)  2.71 us
    pallas_call x1, Pallas kernels, taps_of(): pl.pallas_call(taps_body, grid=(frames,), in_specs=[pl.BlockSpec((1, cell...  1.53 us
  transfers between devices with their start and end apart: 2, of which 1 were waited for; matrix products, arithmetic and copies ran while one was open for 0% of the time, Pallas kernels for 13%

profile of v4, /device:TPU:1, one launch (start us, length us, event | category | flops | bytes accessed | tf_op | source)
XLA Modules:
  0.0 61.4 jit_solution(2347347984118849122)
XLA Ops:
  0.0 1.1 %slice.3 = bf16[2,512,256]{2,1,0:T(8,128)(2,1)S(1)} slice(bf16[4,512,256]{2,1,0:T(8,128)(2,1)} %refs_2_.3), slice={[2:4], [0:512], [0:256]} | slice | bytes 1048576 | tf_op jit(solution)/shard_map/slice | solution.py:176
  1.1 4.5 %collective-permute-start.1 = (bf16[2,512,256]{2,1,0:T(8,128)(2,1)S(1)}, bf16[2,512,256]{2,1,0:T(8,128)(2,1)S(1)}, u32[]{:S(2)}, u32[]{:S(2)}) collective-permute-start(bf16[2,512,256]{2,1,0:T(8,128)(2,1)S(1)} %slice.3), channel_id=1, source_target_pairs={{0,1},{1,2},{2,3},{3,4},{4,5},{5,6},{6,7},{7,8},{8,9},{9,10},{10,1... | collective-permute-start | bytes 1572872 | tf_op jit(solution)/shard_map/ppermute | solution.py:19
  5.6 0.0 copy-start
  5.6 1.2 %copy-done = bf16[4,512,256]{2,1,0:T(8,128)(2,1)S(1)} copy-done((bf16[4,512,256]{2,1,0:T(8,128)(2,1)S(1)}, bf16[4,512,256]{2,1,0:T(8,128)(2,1)}, u32[]{:S(2)}) %copy-start) | copy-done | bytes 1048600
  6.8 0.0 copy-start.1
  6.8 0.7 %copy-done.1 = f32[256]{0:T(256)S(1)} copy-done((f32[256]{0:T(256)S(1)}, f32[256]{0:T(256)}, u32[]{:S(2)}) %copy-start.1) | copy-done | bytes 1048
  7.5 0.0 copy-start.2
  7.5 1.5 %shard_map.64.refs_0_.refs_1_ = bf16[4,4,128,768]{3,2,1,0:T(8,128)(2,1)S(1)} custom-call(bf16[4,512,256]{2,1,0:T(8,128)(2,1)S(1)} %copy-done, f32[1,256]{1,0:T(1,128)S(1)} %bitcast.5), custom_call_target="tpu_custom_call" | custom-call | flops 10485760 | bytes 4194304 | tf_op jit(solution)/shard_map/pallas_call | solution.py:50
  9.1 0.5 copy-done.2
  9.5 3.2 %shard_map.65.refs_2_ = bf16[2,512,256]{2,1,0:T(8,128)(2,1)S(1)} custom-call(bf16[4,4,128,768]{3,2,1,0:T(8,128)(2,1)S(1)} %shard_map.64.refs_0_.refs_1_, bf16[4,4,128,768]{3,2,1,0:T(8,128)(2,1)S(1)} %shard_map.64.refs_0_.refs_1_, bf16[4,512,256]{2,1,0:T(8,128)(2,1)S(1)} %copy-done, f32[1,256]{1,0:T(1,128)S(1)} %bitcast.6, bf16[3,3,768,256]{3,2,1,0:T(8,128)(2,1)S(1)} %bitcast.8), custom_call_target="tpu_custom_call" | custom-call | flops 3623878656 | bytes 3538944 | tf_op jit(solution)/shard_map/pallas_call | solution.py:154
  12.7 0.0 copy-start.3
  12.8 0.0 copy-start.4
  12.8 0.0 copy-start.5
  12.8 2.2 %collective-permute-start = (bf16[2,512,256]{2,1,0:T(8,128)(2,1)S(1)}, bf16[2,512,256]{2,1,0:T(8,128)(2,1)S(1)}, u32[]{:S(2)}, u32[]{:S(2)}) collective-permute-start(bf16[2,512,256]{2,1,0:T(8,128)(2,1)S(1)} %shard_map.65.refs_2_), channel_id=1, source_target_pairs={{0,1},{1,2},{2,3},{3,4},{4,5},{5,6},{6,7},{7,8},{8,9},{9,10},{10,1... | collective-permute-start | bytes 1572872 | tf_op jit(solution)/shard_map/ppermute | solution.py:19
  15.0 0.0 collective-permute-done.1.refs_0_
  15.0 3.4 %shard_map.66.refs_1_ = bf16[2,512,256]{2,1,0:T(8,128)(2,1)S(1)} custom-call(bf16[2,512,256]{2,1,0:T(8,128)(2,1)S(1)} %collective-permute-done.1.refs_0_, bf16[4,4,128,768]{3,2,1,0:T(8,128)(2,1)S(1)} %shard_map.64.refs_0_.refs_1_, bf16[4,512,256]{2,1,0:T(8,128)(2,1)S(1)} %copy-done, f32[1,256]{1,0:T(1,128)S(1)} %bitcast.7, bf16[3,3,768,256]{3,2,1,0:T(8,128)(2,1)S(1)} %bitcast.9), custom_call_target="tpu_custom_call" | custom-call | flops 3623878656 | bytes 3538944 | tf_op jit(solution)/shard_map/pallas_call | solution.py:154
  18.4 2.7 %collective-permute-done.refs_0_ = bf16[2,512,256]{2,1,0:T(8,128)(2,1)S(1)} collective-permute-done((bf16[2,512,256]{2,1,0:T(8,128)(2,1)S(1)}, bf16[2,512,256]{2,1,0:T(8,128)(2,1)S(1)}, u32[]{:S(2)}, u32[]{:S(2)}) %collective-permute-start) | collective-permute-done | bytes 524320 | tf_op jit(solution)/shard_map/ppermute | solution.py:19
  21.1 0.0 copy-done.3
  21.1 0.0 copy-done.4
  21.1 0.0 copy-done.5
  21.1 7.1 %shard_map.67 = bf16[16,4,32,256]{3,2,1,0:T(8,128)(2,1)S(1)} custom-call(bf16[2,512,256]{2,1,0:T(8,128)(2,1)S(1)} %collective-permute-done.refs_0_, bf16[2,512,256]{2,1,0:T(8,128)(2,1)S(1)} %shard_map.66.refs_1_, bf16[2,512,256]{2,1,0:T(8,128)(2,1)S(1)} %shard_map.65.refs_2_, f32[1,256]{1,0:T(1,128)S(1)} %bitcast.11, bf16[3,3,768,256]{3,2,1,0:T(8,128)(2,1)S(1)} %bitcast.10, ...), custom_call_target="tpu_custom_call" | custom-call | flops 7247757312 | bytes 3538944 | tf_op jit(solution)/shard_map/pallas_call | solution.py:154
  28.2 32.2 %all_to_all.5 = bf16[16,4,32,256]{3,2,1,0:T(8,128)(2,1)S(1)} all-to-all(bf16[16,4,32,256]{3,2,1,0:T(8,128)(2,1)S(1)} %shard_map.67), channel_id=1, replica_groups=mesh['clip'=2,'tm'=16] {'tm'}, dimensions={0} | all-to-all | bytes 2097152 | tf_op jit(solution)/shard_map/all_to_all | solution.py:190
  60.5 1.0 %copy.8 = bf16[64,32,256]{2,1,0:T(8,128)(2,1)} copy(bf16[64,32,256]{2,1,0:T(8,128)(2,1)S(1)} %bitcast.12) | data formatting | bytes 2097152
Async XLA Ops:
  1.1 13.9 %collective-permute-start.1 = (bf16[2,512,256]{2,1,0:T(8,128)(2,1)S(1)}, bf16[2,512,256]{2,1,0:T(8,128)(2,1)S(1)}, u32[]{:S(2)}, u32[]{:S(2)}) collective-permute-start(bf16[2,512,256]{2,1,0:T(8,128)(2,1)S(1)} %slice.3), channel_id=1, source_target_pairs={{0,1},{1,2},{2,3},{3,4},{4,5},{5,6},{6,7},{7,8},{8,9},{9,10},{10,1... | collective-permute-start | bytes 1572872 | tf_op jit(solution)/shard_map/ppermute | solution.py:19
  5.6 1.2 %copy-start = (bf16[4,512,256]{2,1,0:T(8,128)(2,1)S(1)}, bf16[4,512,256]{2,1,0:T(8,128)(2,1)}, u32[]{:S(2)}) copy-start(bf16[4,512,256]{2,1,0:T(8,128)(2,1)} %refs_2_.3) | copy-start | bytes 3145732
  6.8 0.7 %copy-start.1 = (f32[256]{0:T(256)S(1)}, f32[256]{0:T(256)}, u32[]{:S(2)}) copy-start(f32[256]{0:T(256)} %param.7) | copy-start | bytes 3076
  7.5 2.0 %copy-start.2 = (bf16[3,3,3,256,256]{4,3,2,1,0:T(8,128)(2,1)S(1)}, bf16[3,3,3,256,256]{4,3,2,1,0:T(8,128)(2,1)}, u32[]{:S(2)}) copy-start(bf16[3,3,3,256,256]{4,3,2,1,0:T(8,128)(2,1)} %param.8) | copy-start | bytes 10616836
  12.7 8.3 %copy-start.3 = (bf16[3,3,3,256,256]{4,3,2,1,0:T(8,128)(2,1)S(1)}, bf16[3,3,3,256,256]{4,3,2,1,0:T(8,128)(2,1)}, u32[]{:S(2)}) copy-start(bf16[3,3,3,256,256]{4,3,2,1,0:T(8,128)(2,1)} %param.10) | copy-start | bytes 10616836
  12.8 8.3 %copy-start.4 = (bf16[256,256]{1,0:T(8,128)(2,1)S(1)}, bf16[256,256]{1,0:T(8,128)(2,1)}, u32[]{:S(2)}) copy-start(bf16[256,256]{1,0:T(8,128)(2,1)} %refs_5_.1) | copy-start | bytes 393220
  12.8 8.3 %copy-start.5 = (f32[256]{0:T(256)S(1)}, f32[256]{0:T(256)}, u32[]{:S(2)}) copy-start(f32[256]{0:T(256)} %param.9) | copy-start | bytes 3076
  12.8 8.3 %collective-permute-start = (bf16[2,512,256]{2,1,0:T(8,128)(2,1)S(1)}, bf16[2,512,256]{2,1,0:T(8,128)(2,1)S(1)}, u32[]{:S(2)}, u32[]{:S(2)}) collective-permute-start(bf16[2,512,256]{2,1,0:T(8,128)(2,1)S(1)} %shard_map.65.refs_2_), channel_id=1, source_target_pairs={{0,1},{1,2},{2,3},{3,4},{4,5},{5,6},{6,7},{7,8},{8,9},{9,10},{10,1... | collective-permute-start | bytes 1572872 | tf_op jit(solution)/shard_map/ppermute | solution.py:19

commit v5 on v4

--- a/solution.py
+++ b/solution.py
@@ -63,7 +63,7 @@
     )(x, gain.reshape(1, channels))
 
 
-def conv_body(ready, project, *refs):
+def conv_body(ready, project, onto, *refs):
     groups = len(ready)
     sources, refs = refs[:groups], list(refs[groups:])
     residuals = [refs.pop(0) if ready[g] else sources[g] for g in range(1, groups)]
@@ -71,6 +71,8 @@
     rest = refs[2:]
     if project:
         weight_ref, rest = rest[0], rest[1:]
+    if onto:
+        rest = rest[1:]
     out_ref, taps_ref, sum_ref = rest
     channels = gain_ref.shape[-1]
     gain = gain_ref[...]
@@ -124,7 +126,7 @@
             out_ref[base : base + HALO] = block
 
 
-def conv_block(sources, gain, kernel, weight=None, owners=None):
+def conv_block(sources, gain, kernel, weight=None, owners=None, halves=1, half=0, into=None):
     groups = len(sources)
     ready = tuple(len(source) == 3 for source in sources)
     outcount = HALO * (groups - 1)
@@ -147,15 +149,23 @@
         operands.append(weight)
         specs.append(whole(channels, channels))
     if owners is not None:
-        shape = (owners, outcount, cells // owners, channels)
+        block, index = (owners, outcount, cells // owners, channels), (0, half, 0, 0)
+        shape = (owners, halves * outcount) + block[2:]
     else:
-        shape = (outcount, cells, channels)
+        block, index = (outcount, cells, channels), (half, 0, 0)
+        shape = (halves * outcount,) + block[1:]
+    aliases = {}
+    if into is not None:
+        aliases = {len(operands): 0}
+        operands.append(into)
+        specs.append(pl.BlockSpec(memory_space=pl.ANY))
     flops = 2 * outcount * cells * 27 * channels * channels
     return pl.pallas_call(
-        functools.partial(conv_body, ready, weight is not None),
+        functools.partial(conv_body, ready, weight is not None, into is not None),
         grid=(1,),
         in_specs=specs,
-        out_specs=whole(*shape),
+        out_specs=pl.BlockSpec(block, lambda i: index),
+        input_output_aliases=aliases,
         out_shape=jax.ShapeDtypeStruct(shape, jnp.bfloat16),
         scratch_shapes=[
             pltpu.VMEM((HALO * groups, ROWS, COLS, 3 * channels), jnp.bfloat16),
@@ -179,12 +189,10 @@
     late_earlier = passed_along(late, "tm", 1)
     early = conv_block([(earlier, 0), (frames, 0, taps)], gain_one, conv_one)
     aligned = owned % 16 == 0
+    owners = members if aligned else None
+    projected = conv_block([(early, 0), (late, 0)], gain_two, conv_two, out_weight, owners, halves=2, half=1)
     projected = conv_block(
-        [(late_earlier, 0), (early, 0), (late, 0)],
-        gain_two,
-        conv_two,
-        out_weight,
-        members if aligned else None,
+        [(late_earlier, 0), (early, 0)], gain_two, conv_two, out_weight, owners, halves=2, half=0, into=projected
     )
     if aligned:
         latent = lax.all_to_all(projected, "tm", split_axis=0, concat_axis=0, tiled=True)

time: 61.7 us -> 58.2 us (0.943)
  waiting for transfers between devices: 2.71 us -> 0.01 us
  blocking collectives: 32.2 us -> 31.3 us
    ppermute x2, waiting for transfers between devices: 2.71 us -> 0.01 us  [passed_along(): return lax.ppermute(x, axis, pairs)]
    all_to_all x1, blocking collectives: 32.2 us -> 31.3 us  [body(): lax.all_to_all(projected, 'tm', split_axis=0, concat_axis=0, tiled=True)]
    pallas_call x3 -> x4, Pallas kernels: 13.7 us -> 13.8 us  [conv_block(): pl.pallas_call(functools.partial(conv_body, ready, weight is not None, in...]
  transfers between devices with their start and end apart: 2 -> 2, of which waited for: 1 -> 0; matrix products, arithmetic and copies ran while one was open for 0% -> 0% of each run, Pallas kernels for 13% -> 20%
where the time goes in v5:
time: 58.2 us; the launch traced here: 57.9 us
  blocking collectives  31.3 us (54%)
  Pallas kernels  15.3 us (26%)
  starting transfers between devices  6.71 us (12%)
  local copies, waits for them, and re-layouts  4.43 us (8%)
    all_to_all x1, blocking collectives, body(): lax.all_to_all(projected, 'tm', split_axis=0, concat_axis=0, tiled=True)  31.3 us
    pallas_call x4, Pallas kernels, conv_block(): pl.pallas_call(functools.partial(conv_body, ready, weight is not None, in...  13.8 us
    ppermute x2, starting transfers between devices, passed_along(): return lax.ppermute(x, axis, pairs)  6.71 us
    unnamed x13, local copies, waits for them, and re-layouts  3.35 us
    pallas_call x1, Pallas kernels, taps_of(): pl.pallas_call(taps_body, grid=(frames,), in_specs=[pl.BlockSpec((1, cell...  1.53 us
  transfers between devices with their start and end apart: 2, of which 0 were waited for; matrix products, arithmetic and copies ran while one was open for 0% of the time, Pallas kernels for 20%

profile of v5, /device:TPU:1, one launch (start us, length us, event | category | flops | bytes accessed | tf_op | source)
XLA Modules:
  0.0 57.9 jit_solution(6211230351135824486)
XLA Ops:
  0.0 1.1 %slice.3 = bf16[2,512,256]{2,1,0:T(8,128)(2,1)S(1)} slice(bf16[4,512,256]{2,1,0:T(8,128)(2,1)} %refs_2_.3), slice={[2:4], [0:512], [0:256]} | slice | bytes 1048576 | tf_op jit(solution)/shard_map/slice | solution.py:186
  1.1 4.5 %collective-permute-start.1 = (bf16[2,512,256]{2,1,0:T(8,128)(2,1)S(1)}, bf16[2,512,256]{2,1,0:T(8,128)(2,1)S(1)}, u32[]{:S(2)}, u32[]{:S(2)}) collective-permute-start(bf16[2,512,256]{2,1,0:T(8,128)(2,1)S(1)} %slice.3), channel_id=1, source_target_pairs={{0,1},{1,2},{2,3},{3,4},{4,5},{5,6},{6,7},{7,8},{8,9},{9,10},{10,1... | collective-permute-start | bytes 1572872 | tf_op jit(solution)/shard_map/ppermute | solution.py:19
  5.6 0.0 copy-start
  5.6 1.2 %copy-done = bf16[4,512,256]{2,1,0:T(8,128)(2,1)S(1)} copy-done((bf16[4,512,256]{2,1,0:T(8,128)(2,1)S(1)}, bf16[4,512,256]{2,1,0:T(8,128)(2,1)}, u32[]{:S(2)}) %copy-start) | copy-done | bytes 1048600
  6.8 0.0 copy-start.1
  6.8 0.7 %copy-done.1 = f32[256]{0:T(256)S(1)} copy-done((f32[256]{0:T(256)S(1)}, f32[256]{0:T(256)}, u32[]{:S(2)}) %copy-start.1) | copy-done | bytes 1048
  7.5 0.0 copy-start.2
  7.5 1.5 %shard_map.64.refs_0_.refs_1_ = bf16[4,4,128,768]{3,2,1,0:T(8,128)(2,1)S(1)} custom-call(bf16[4,512,256]{2,1,0:T(8,128)(2,1)S(1)} %copy-done, f32[1,256]{1,0:T(1,128)S(1)} %bitcast.5), custom_call_target="tpu_custom_call" | custom-call | flops 10485760 | bytes 4194304 | tf_op jit(solution)/shard_map/pallas_call | solution.py:50
  9.1 0.5 copy-done.2
  9.5 3.2 %shard_map.65.refs_1_ = bf16[2,512,256]{2,1,0:T(8,128)(2,1)S(1)} custom-call(bf16[4,4,128,768]{3,2,1,0:T(8,128)(2,1)S(1)} %shard_map.64.refs_0_.refs_1_, bf16[4,4,128,768]{3,2,1,0:T(8,128)(2,1)S(1)} %shard_map.64.refs_0_.refs_1_, bf16[4,512,256]{2,1,0:T(8,128)(2,1)S(1)} %copy-done, f32[1,256]{1,0:T(1,128)S(1)} %bitcast.6, bf16[3,3,768,256]{3,2,1,0:T(8,128)(2,1)S(1)} %bitcast.8), custom_call_target="tpu_custom_call" | custom-call | flops 3623878656 | bytes 3538944 | tf_op jit(solution)/shard_map/pallas_call | solution.py:163
  12.7 0.0 copy-start.3
  12.8 0.0 copy-start.4
  12.8 0.0 copy-start.5
  12.8 2.2 %collective-permute-start = (bf16[2,512,256]{2,1,0:T(8,128)(2,1)S(1)}, bf16[2,512,256]{2,1,0:T(8,128)(2,1)S(1)}, u32[]{:S(2)}, u32[]{:S(2)}) collective-permute-start(bf16[2,512,256]{2,1,0:T(8,128)(2,1)S(1)} %shard_map.65.refs_1_), channel_id=1, source_target_pairs={{0,1},{1,2},{2,3},{3,4},{4,5},{5,6},{6,7},{7,8},{8,9},{9,10},{10,1... | collective-permute-start | bytes 1572872 | tf_op jit(solution)/shard_map/ppermute | solution.py:19
  15.0 0.0 collective-permute-done.1.refs_0_
  15.0 3.4 %shard_map.66.refs_0_.refs_1_ = bf16[2,512,256]{2,1,0:T(8,128)(2,1)S(1)} custom-call(bf16[2,512,256]{2,1,0:T(8,128)(2,1)S(1)} %collective-permute-done.1.refs_0_, bf16[4,4,128,768]{3,2,1,0:T(8,128)(2,1)S(1)} %shard_map.64.refs_0_.refs_1_, bf16[4,512,256]{2,1,0:T(8,128)(2,1)S(1)} %copy-done, f32[1,256]{1,0:T(1,128)S(1)} %bitcast.7, ...), custom_call_target="tpu_custom_call" | custom-call | flops 3623878656 | bytes 3538944 | tf_op jit(solution)/shard_map/pallas_call | solution.py:163
  18.4 0.0 copy-done.3
  18.4 0.0 copy-done.4
  18.4 0.0 copy-done.5
  18.4 3.6 %shard_map.67.refs_5_ = bf16[16,4,32,256]{3,2,1,0:T(8,128)(2,1)S(1)} custom-call(bf16[2,512,256]{2,1,0:T(8,128)(2,1)S(1)} %shard_map.66.refs_0_.refs_1_, bf16[2,512,256]{2,1,0:T(8,128)(2,1)S(1)} %shard_map.65.refs_1_, f32[1,256]{1,0:T(1,128)S(1)} %bitcast.12, bf16[3,3,768,256]{3,2,1,0:T(8,128)(2,1)S(1)} %bitcast.10, bf16[256,256]{1,0:T(8,128)(2,1)S(1)} %copy-done.4), custom_call_target="tpu_custom_call" | custom-call | flops 3623878656 | bytes 3538944 | tf_op jit(solution)/shard_map/pallas_call | solution.py:163
  22.0 0.0 collective-permute-done.refs_0_
  22.0 3.6 %shard_map.68 = bf16[16,4,32,256]{3,2,1,0:T(8,128)(2,1)S(1)} custom-call(bf16[2,512,256]{2,1,0:T(8,128)(2,1)S(1)} %collective-permute-done.refs_0_, bf16[2,512,256]{2,1,0:T(8,128)(2,1)S(1)} %shard_map.66.refs_0_.refs_1_, f32[1,256]{1,0:T(1,128)S(1)} %bitcast.13, bf16[3,3,768,256]{3,2,1,0:T(8,128)(2,1)S(1)} %bitcast.11, ...), custom_call_target="tpu_custom_call", output_to_operand_aliasing={{}: (5, {})} | custom-call | flops 3623878656 | bytes 3538944 | tf_op jit(solution)/shard_map/pallas_call | solution.py:163
  25.6 31.3 %all_to_all.5 = bf16[16,4,32,256]{3,2,1,0:T(8,128)(2,1)S(1)} all-to-all(bf16[16,4,32,256]{3,2,1,0:T(8,128)(2,1)S(1)} %shard_map.68), channel_id=1, replica_groups=mesh['clip'=2,'tm'=16] {'tm'}, dimensions={0} | all-to-all | bytes 2097152 | tf_op jit(solution)/shard_map/all_to_all | solution.py:198
  56.9 1.0 %copy.10 = bf16[64,32,256]{2,1,0:T(8,128)(2,1)} copy(bf16[64,32,256]{2,1,0:T(8,128)(2,1)S(1)} %bitcast.14) | data formatting | bytes 2097152
Async XLA Ops:
  1.1 13.9 %collective-permute-start.1 = (bf16[2,512,256]{2,1,0:T(8,128)(2,1)S(1)}, bf16[2,512,256]{2,1,0:T(8,128)(2,1)S(1)}, u32[]{:S(2)}, u32[]{:S(2)}) collective-permute-start(bf16[2,512,256]{2,1,0:T(8,128)(2,1)S(1)} %slice.3), channel_id=1, source_target_pairs={{0,1},{1,2},{2,3},{3,4},{4,5},{5,6},{6,7},{7,8},{8,9},{9,10},{10,1... | collective-permute-start | bytes 1572872 | tf_op jit(solution)/shard_map/ppermute | solution.py:19
  5.6 1.2 %copy-start = (bf16[4,512,256]{2,1,0:T(8,128)(2,1)S(1)}, bf16[4,512,256]{2,1,0:T(8,128)(2,1)}, u32[]{:S(2)}) copy-start(bf16[4,512,256]{2,1,0:T(8,128)(2,1)} %refs_2_.3) | copy-start | bytes 3145732
  6.8 0.7 %copy-start.1 = (f32[256]{0:T(256)S(1)}, f32[256]{0:T(256)}, u32[]{:S(2)}) copy-start(f32[256]{0:T(256)} %param.7) | copy-start | bytes 3076
  7.5 2.0 %copy-start.2 = (bf16[3,3,3,256,256]{4,3,2,1,0:T(8,128)(2,1)S(1)}, bf16[3,3,3,256,256]{4,3,2,1,0:T(8,128)(2,1)}, u32[]{:S(2)}) copy-start(bf16[3,3,3,256,256]{4,3,2,1,0:T(8,128)(2,1)} %param.8) | copy-start | bytes 10616836
  12.7 5.6 %copy-start.3 = (bf16[3,3,3,256,256]{4,3,2,1,0:T(8,128)(2,1)S(1)}, bf16[3,3,3,256,256]{4,3,2,1,0:T(8,128)(2,1)}, u32[]{:S(2)}) copy-start(bf16[3,3,3,256,256]{4,3,2,1,0:T(8,128)(2,1)} %param.10) | copy-start | bytes 10616836
  12.8 5.6 %copy-start.4 = (bf16[256,256]{1,0:T(8,128)(2,1)S(1)}, bf16[256,256]{1,0:T(8,128)(2,1)}, u32[]{:S(2)}) copy-start(bf16[256,256]{1,0:T(8,128)(2,1)} %refs_4_.3) | copy-start | bytes 393220
  12.8 5.6 %copy-start.5 = (f32[256]{0:T(256)S(1)}, f32[256]{0:T(256)}, u32[]{:S(2)}) copy-start(f32[256]{0:T(256)} %param.9) | copy-start | bytes 3076
  12.8 9.2 %collective-permute-start = (bf16[2,512,256]{2,1,0:T(8,128)(2,1)S(1)}, bf16[2,512,256]{2,1,0:T(8,128)(2,1)S(1)}, u32[]{:S(2)}, u32[]{:S(2)}) collective-permute-start(bf16[2,512,256]{2,1,0:T(8,128)(2,1)S(1)} %shard_map.65.refs_1_), channel_id=1, source_target_pairs={{0,1},{1,2},{2,3},{3,4},{4,5},{5,6},{6,7},{7,8},{8,9},{9,10},{10,1... | collective-permute-start | bytes 1572872 | tf_op jit(solution)/shard_map/ppermute | solution.py:19

commit v6 on v5

--- a/solution.py
+++ b/solution.py
@@ -61,6 +61,25 @@
             flops=20 * frames * cells * channels, bytes_accessed=8 * frames * cells * channels, transcendentals=0
         ),
     )(x, gain.reshape(1, channels))
+
+
+def copy_body(source, out_ref):
+    out_ref[...] = source[...]
+
+
+def last_frames(x):
+    frames, cells, channels = x.shape
+    return pl.pallas_call(
+        copy_body,
+        grid=(1,),
+        in_specs=[pl.BlockSpec((HALO, cells, channels), lambda i: (frames // HALO - 1, 0, 0))],
+        out_specs=pl.BlockSpec((HALO, cells, channels), lambda i: (0, 0, 0)),
+        out_shape=jax.ShapeDtypeStruct((HALO, cells, channels), x.dtype),
+        compiler_params=pltpu.CompilerParams(vmem_limit_bytes=VMEM_LIMIT),
+        cost_estimate=pl.CostEstimate(
+            flops=HALO * cells * channels, bytes_accessed=4 * HALO * cells * channels, transcendentals=0
+        ),
+    )(x)
 
 
 def conv_body(ready, project, onto, *refs):
@@ -183,7 +202,7 @@
     members = lax.axis_size("tm")
     owned = cells // members
     assert local_frames == 2 * HALO
-    earlier = passed_along(frames[-HALO:], "tm", 1)
+    earlier = passed_along(last_frames(frames), "tm", 1)
     taps = taps_of(frames, gain_one)
     late = conv_block([(frames, 0, taps), (frames, 1, taps)], gain_one, conv_one)
     late_earlier = passed_along(late, "tm", 1)

time: 58.2 us -> 57.1 us (0.981)
  local copies, waits for them, and re-layouts: 4.43 us -> 3.35 us
    slice x1 -> x0, local copies, waits for them, and re-layouts: 1.08 us -> none  [body(): earlier = passed_along(frames[-HALO:], 'tm', 1)]
  transfers between devices with their start and end apart: 2 -> 2, of which waited for: 0 -> 0; matrix products, arithmetic and copies ran while one was open for 0% -> 0% of each run, Pallas kernels for 20% -> 21%
where the time goes in v6:
time: 57.1 us; the launch traced here: 56.8 us
  blocking collectives  31.3 us (55%)
  Pallas kernels  15.4 us (27%)
  starting transfers between devices  6.71 us (12%)
  local copies, waits for them, and re-layouts  3.35 us (6%)
    all_to_all x1, blocking collectives, body(): lax.all_to_all(projected, 'tm', split_axis=0, concat_axis=0, tiled=True)  31.3 us
    pallas_call x4, Pallas kernels, conv_block(): pl.pallas_call(functools.partial(conv_body, ready, weight is not None, in...  13.8 us
    ppermute x2, starting transfers between devices, passed_along(): return lax.ppermute(x, axis, pairs)  6.71 us
    unnamed x13, local copies, waits for them, and re-layouts  3.35 us
    pallas_call x1, Pallas kernels, taps_of(): pl.pallas_call(taps_body, grid=(frames,), in_specs=[pl.BlockSpec((1, cell...  1.53 us
  transfers between devices with their start and end apart: 2, of which 0 were waited for; matrix products, arithmetic and copies ran while one was open for 0% of the time, Pallas kernels for 21%

profile of v6, /device:TPU:1, one launch (start us, length us, event | category | flops | bytes accessed | tf_op | source)
XLA Modules:
  0.0 56.8 jit_solution(4223216612434165056)
XLA Ops:
  0.0 0.0 copy-start
  0.0 1.2 %copy-done = bf16[4,512,256]{2,1,0:T(8,128)(2,1)S(1)} copy-done((bf16[4,512,256]{2,1,0:T(8,128)(2,1)S(1)}, bf16[4,512,256]{2,1,0:T(8,128)(2,1)}, u32[]{:S(2)}) %copy-start) | copy-done | bytes 1048600
  1.3 4.5 %collective-permute-start.1 = (bf16[2,512,256]{2,1,0:T(8,128)(2,1)S(1)}, bf16[2,512,256]{2,1,0:T(8,128)(2,1)S(1)}, u32[]{:S(2)}, u32[]{:S(2)}) collective-permute-start(bf16[2,512,256]{2,1,0:T(8,128)(2,1)S(1)} %shard_map.66), channel_id=1, source_target_pairs={{0,1},{1,2},{2,3},{3,4},{4,5},{5,6},{6,7},{7,8},{8,9},{9,10},{10,1... | collective-permute-start | bytes 1572872 | tf_op jit(solution)/shard_map/ppermute | solution.py:19
  5.8 0.0 copy-start.1
  5.8 0.7 %copy-done.1 = f32[256]{0:T(256)S(1)} copy-done((f32[256]{0:T(256)S(1)}, f32[256]{0:T(256)}, u32[]{:S(2)}) %copy-start.1) | copy-done | bytes 1048
  6.5 0.0 copy-start.2
  6.5 1.5 %shard_map.64.refs_0_.refs_1_ = bf16[4,4,128,768]{3,2,1,0:T(8,128)(2,1)S(1)} custom-call(bf16[4,512,256]{2,1,0:T(8,128)(2,1)S(1)} %copy-done, f32[1,256]{1,0:T(1,128)S(1)} %bitcast.5), custom_call_target="tpu_custom_call" | custom-call | flops 10485760 | bytes 4194304 | tf_op jit(solution)/shard_map/pallas_call | solution.py:50
  8.0 0.5 copy-done.2
  8.5 3.2 %shard_map.65.refs_1_ = bf16[2,512,256]{2,1,0:T(8,128)(2,1)S(1)} custom-call(bf16[4,4,128,768]{3,2,1,0:T(8,128)(2,1)S(1)} %shard_map.64.refs_0_.refs_1_, bf16[4,4,128,768]{3,2,1,0:T(8,128)(2,1)S(1)} %shard_map.64.refs_0_.refs_1_, bf16[4,512,256]{2,1,0:T(8,128)(2,1)S(1)} %copy-done, f32[1,256]{1,0:T(1,128)S(1)} %bitcast.6, bf16[3,3,768,256]{3,2,1,0:T(8,128)(2,1)S(1)} %bitcast.8), custom_call_target="tpu_custom_call" | custom-call | flops 3623878656 | bytes 3538944 | tf_op jit(solution)/shard_map/pallas_call | solution.py:182
  11.7 0.0 copy-start.3
  11.7 0.0 copy-start.4
  11.7 0.0 copy-start.5
  11.7 2.2 %collective-permute-start = (bf16[2,512,256]{2,1,0:T(8,128)(2,1)S(1)}, bf16[2,512,256]{2,1,0:T(8,128)(2,1)S(1)}, u32[]{:S(2)}, u32[]{:S(2)}) collective-permute-start(bf16[2,512,256]{2,1,0:T(8,128)(2,1)S(1)} %shard_map.65.refs_1_), channel_id=1, source_target_pairs={{0,1},{1,2},{2,3},{3,4},{4,5},{5,6},{6,7},{7,8},{8,9},{9,10},{10,1... | collective-permute-start | bytes 1572872 | tf_op jit(solution)/shard_map/ppermute | solution.py:19
  13.9 0.0 collective-permute-done.1.refs_0_
  13.9 3.4 %shard_map.67.refs_0_.refs_1_ = bf16[2,512,256]{2,1,0:T(8,128)(2,1)S(1)} custom-call(bf16[2,512,256]{2,1,0:T(8,128)(2,1)S(1)} %collective-permute-done.1.refs_0_, bf16[4,4,128,768]{3,2,1,0:T(8,128)(2,1)S(1)} %shard_map.64.refs_0_.refs_1_, bf16[4,512,256]{2,1,0:T(8,128)(2,1)S(1)} %copy-done, f32[1,256]{1,0:T(1,128)S(1)} %bitcast.7, ...), custom_call_target="tpu_custom_call" | custom-call | flops 3623878656 | bytes 3538944 | tf_op jit(solution)/shard_map/pallas_call | solution.py:182
  17.3 0.0 copy-done.3
  17.3 0.0 copy-done.4
  17.3 0.0 copy-done.5
  17.4 3.6 %shard_map.68.refs_5_ = bf16[16,4,32,256]{3,2,1,0:T(8,128)(2,1)S(1)} custom-call(bf16[2,512,256]{2,1,0:T(8,128)(2,1)S(1)} %shard_map.67.refs_0_.refs_1_, bf16[2,512,256]{2,1,0:T(8,128)(2,1)S(1)} %shard_map.65.refs_1_, f32[1,256]{1,0:T(1,128)S(1)} %bitcast.12, bf16[3,3,768,256]{3,2,1,0:T(8,128)(2,1)S(1)} %bitcast.10, bf16[256,256]{1,0:T(8,128)(2,1)S(1)} %copy-done.4), custom_call_target="tpu_custom_call" | custom-call | flops 3623878656 | bytes 3538944 | tf_op jit(solution)/shard_map/pallas_call | solution.py:182
  21.0 0.0 collective-permute-done.refs_0_
  21.0 3.6 %shard_map.69 = bf16[16,4,32,256]{3,2,1,0:T(8,128)(2,1)S(1)} custom-call(bf16[2,512,256]{2,1,0:T(8,128)(2,1)S(1)} %collective-permute-done.refs_0_, bf16[2,512,256]{2,1,0:T(8,128)(2,1)S(1)} %shard_map.67.refs_0_.refs_1_, f32[1,256]{1,0:T(1,128)S(1)} %bitcast.13, bf16[3,3,768,256]{3,2,1,0:T(8,128)(2,1)S(1)} %bitcast.11, ...), custom_call_target="tpu_custom_call", output_to_operand_aliasing={{}: (5, {})} | custom-call | flops 3623878656 | bytes 3538944 | tf_op jit(solution)/shard_map/pallas_call | solution.py:182
  24.6 31.3 %all_to_all.5 = bf16[16,4,32,256]{3,2,1,0:T(8,128)(2,1)S(1)} all-to-all(bf16[16,4,32,256]{3,2,1,0:T(8,128)(2,1)S(1)} %shard_map.69), channel_id=1, replica_groups=mesh['clip'=2,'tm'=16] {'tm'}, dimensions={0} | all-to-all | bytes 2097152 | tf_op jit(solution)/shard_map/all_to_all | solution.py:217
  55.9 1.0 %copy.10 = bf16[64,32,256]{2,1,0:T(8,128)(2,1)} copy(bf16[64,32,256]{2,1,0:T(8,128)(2,1)S(1)} %bitcast.14) | data formatting | bytes 2097152
  (1 shorter events, 0.0 us)
Async XLA Ops:
  0.0 1.2 %copy-start = (bf16[4,512,256]{2,1,0:T(8,128)(2,1)S(1)}, bf16[4,512,256]{2,1,0:T(8,128)(2,1)}, u32[]{:S(2)}) copy-start(bf16[4,512,256]{2,1,0:T(8,128)(2,1)} %refs_2_.3) | copy-start | bytes 3145732
  1.3 12.7 %collective-permute-start.1 = (bf16[2,512,256]{2,1,0:T(8,128)(2,1)S(1)}, bf16[2,512,256]{2,1,0:T(8,128)(2,1)S(1)}, u32[]{:S(2)}, u32[]{:S(2)}) collective-permute-start(bf16[2,512,256]{2,1,0:T(8,128)(2,1)S(1)} %shard_map.66), channel_id=1, source_target_pairs={{0,1},{1,2},{2,3},{3,4},{4,5},{5,6},{6,7},{7,8},{8,9},{9,10},{10,1... | collective-permute-start | bytes 1572872 | tf_op jit(solution)/shard_map/ppermute | solution.py:19
  5.8 0.7 %copy-start.1 = (f32[256]{0:T(256)S(1)}, f32[256]{0:T(256)}, u32[]{:S(2)}) copy-start(f32[256]{0:T(256)} %param.7) | copy-start | bytes 3076
  6.5 2.0 %copy-start.2 = (bf16[3,3,3,256,256]{4,3,2,1,0:T(8,128)(2,1)S(1)}, bf16[3,3,3,256,256]{4,3,2,1,0:T(8,128)(2,1)}, u32[]{:S(2)}) copy-start(bf16[3,3,3,256,256]{4,3,2,1,0:T(8,128)(2,1)} %param.8) | copy-start | bytes 10616836
  11.7 5.6 %copy-start.3 = (bf16[3,3,3,256,256]{4,3,2,1,0:T(8,128)(2,1)S(1)}, bf16[3,3,3,256,256]{4,3,2,1,0:T(8,128)(2,1)}, u32[]{:S(2)}) copy-start(bf16[3,3,3,256,256]{4,3,2,1,0:T(8,128)(2,1)} %param.10) | copy-start | bytes 10616836
  11.7 5.6 %copy-start.4 = (bf16[256,256]{1,0:T(8,128)(2,1)S(1)}, bf16[256,256]{1,0:T(8,128)(2,1)}, u32[]{:S(2)}) copy-start(bf16[256,256]{1,0:T(8,128)(2,1)} %refs_4_.3) | copy-start | bytes 393220
  11.7 5.6 %copy-start.5 = (f32[256]{0:T(256)S(1)}, f32[256]{0:T(256)}, u32[]{:S(2)}) copy-start(f32[256]{0:T(256)} %param.9) | copy-start | bytes 3076
  11.7 9.2 %collective-permute-start = (bf16[2,512,256]{2,1,0:T(8,128)(2,1)S(1)}, bf16[2,512,256]{2,1,0:T(8,128)(2,1)S(1)}, u32[]{:S(2)}, u32[]{:S(2)}) collective-permute-start(bf16[2,512,256]{2,1,0:T(8,128)(2,1)S(1)} %shard_map.65.refs_1_), channel_id=1, source_target_pairs={{0,1},{1,2},{2,3},{3,4},{4,5},{5,6},{6,7},{7,8},{8,9},{9,10},{10,1... | collective-permute-start | bytes 1572872 | tf_op jit(solution)/shard_map/ppermute | solution.py:19

commit v7 on v6

--- a/solution.py
+++ b/solution.py
@@ -63,23 +63,33 @@
     )(x, gain.reshape(1, channels))
 
 
-def copy_body(source, out_ref):
+def copy_body(source, gain_ref, out_ref, gain_out_ref):
     out_ref[...] = source[...]
-
-
-def last_frames(x):
+    gain_out_ref[...] = gain_ref[...]
+
+
+def last_frames(x, gain):
     frames, cells, channels = x.shape
     return pl.pallas_call(
         copy_body,
         grid=(1,),
-        in_specs=[pl.BlockSpec((HALO, cells, channels), lambda i: (frames // HALO - 1, 0, 0))],
-        out_specs=pl.BlockSpec((HALO, cells, channels), lambda i: (0, 0, 0)),
-        out_shape=jax.ShapeDtypeStruct((HALO, cells, channels), x.dtype),
+        in_specs=[
+            pl.BlockSpec((HALO, cells, channels), lambda i: (frames // HALO - 1, 0, 0)),
+            pl.BlockSpec((1, channels), lambda i: (0, 0)),
+        ],
+        out_specs=[
+            pl.BlockSpec((HALO, cells, channels), lambda i: (0, 0, 0)),
+            pl.BlockSpec((1, channels), lambda i: (0, 0)),
+        ],
+        out_shape=[
+            jax.ShapeDtypeStruct((HALO, cells, channels), x.dtype),
+            jax.ShapeDtypeStruct((1, channels), gain.dtype),
+        ],
         compiler_params=pltpu.CompilerParams(vmem_limit_bytes=VMEM_LIMIT),
         cost_estimate=pl.CostEstimate(
             flops=HALO * cells * channels, bytes_accessed=4 * HALO * cells * channels, transcendentals=0
         ),
-    )(x)
+    )(x, gain.reshape(1, channels))
 
 
 def conv_body(ready, project, onto, *refs):
@@ -202,7 +212,8 @@
     members = lax.axis_size("tm")
     owned = cells // members
     assert local_frames == 2 * HALO
-    earlier = passed_along(last_frames(frames), "tm", 1)
+    tail, gain_one = last_frames(frames, gain_one)
+    earlier = passed_along(tail, "tm", 1)
     taps = taps_of(frames, gain_one)
     late = conv_block([(frames, 0, taps), (frames, 1, taps)], gain_one, conv_one)
     late_earlier = passed_along(late, "tm", 1)

time: 57.1 us -> 56.9 us (level)
  no operation moved by 1% of the time
where the time goes in v7:
time: 56.9 us; the launch traced here: 56.7 us
  blocking collectives  31.3 us (55%)
  Pallas kernels  15.4 us (27%)
  starting transfers between devices  6.97 us (12%)
  local copies, waits for them, and re-layouts  2.9 us (5%)
    all_to_all x1, blocking collectives, body(): lax.all_to_all(projected, 'tm', split_axis=0, concat_axis=0, tiled=True)  31.3 us
    pallas_call x4, Pallas kernels, conv_block(): pl.pallas_call(functools.partial(conv_body, ready, weight is not None, in...  13.8 us
    ppermute x2, starting transfers between devices, passed_along(): return lax.ppermute(x, axis, pairs)  6.97 us
    unnamed x13, local copies, waits for them, and re-layouts  2.9 us
    pallas_call x1, Pallas kernels, taps_of(): pl.pallas_call(taps_body, grid=(frames,), in_specs=[pl.BlockSpec((1, cell...  1.55 us
  transfers between devices with their start and end apart: 2, of which 0 were waited for; matrix products, arithmetic and copies ran while one was open for 0% of the time, Pallas kernels for 21%

profile of v7, /device:TPU:1, one launch (start us, length us, event | category | flops | bytes accessed | tf_op | source)
XLA Modules:
  0.0 56.7 jit_solution(2793475454054741494)
XLA Ops:
  0.0 0.0 copy-start
  0.0 1.2 %copy-done = bf16[4,512,256]{2,1,0:T(8,128)(2,1)S(1)} copy-done((bf16[4,512,256]{2,1,0:T(8,128)(2,1)S(1)}, bf16[4,512,256]{2,1,0:T(8,128)(2,1)}, u32[]{:S(2)}) %copy-start) | copy-done | bytes 1048600
  1.2 0.0 copy-start.1
  1.2 0.7 %copy-done.1 = f32[256]{0:T(256)S(1)} copy-done((f32[256]{0:T(256)S(1)}, f32[256]{0:T(256)}, u32[]{:S(2)}) %copy-start.1) | copy-done | bytes 1048
  1.9 0.0 copy-start.2
  1.9 4.8 %collective-permute-start.1 = (bf16[2,512,256]{2,1,0:T(8,128)(2,1)S(1)}, bf16[2,512,256]{2,1,0:T(8,128)(2,1)S(1)}, u32[]{:S(2)}, u32[]{:S(2)}) collective-permute-start(bf16[2,512,256]{2,1,0:T(8,128)(2,1)S(1)} %get-tuple-element.8), channel_id=1, source_target_pairs={{0,1},{1,2},{2,3},{3,4},{4,5},{5,6},{6,7},{7,8},{8,9},{9,10},{10,1... | collective-permute-start | bytes 1572872 | tf_op jit(solution)/shard_map/ppermute | solution.py:19
  6.7 1.5 %shard_map.65.refs_0_.refs_1_ = bf16[4,4,128,768]{3,2,1,0:T(8,128)(2,1)S(1)} custom-call(bf16[4,512,256]{2,1,0:T(8,128)(2,1)S(1)} %copy-done, f32[1,256]{1,0:T(1,128)S(1)} %get-tuple-element.7.gain_ref.refs_3_), custom_call_target="tpu_custom_call" | custom-call | flops 10485760 | bytes 4194304 | tf_op jit(solution)/shard_map/pallas_call | solution.py:50
  8.3 0.0 copy-done.2
  8.3 3.2 %shard_map.66.refs_1_ = bf16[2,512,256]{2,1,0:T(8,128)(2,1)S(1)} custom-call(bf16[4,4,128,768]{3,2,1,0:T(8,128)(2,1)S(1)} %shard_map.65.refs_0_.refs_1_, bf16[4,4,128,768]{3,2,1,0:T(8,128)(2,1)S(1)} %shard_map.65.refs_0_.refs_1_, bf16[4,512,256]{2,1,0:T(8,128)(2,1)S(1)} %copy-done, f32[1,256]{1,0:T(1,128)S(1)} %get-tuple-element.7.gain_ref.refs_3_, ...), custom_call_target="tpu_custom_call" | custom-call | flops 3623878656 | bytes 3538944 | tf_op jit(solution)/shard_map/pallas_call | solution.py:192
  11.5 0.0 copy-start.3
  11.5 0.0 copy-start.4
  11.6 0.0 copy-start.5
  11.6 2.2 %collective-permute-start = (bf16[2,512,256]{2,1,0:T(8,128)(2,1)S(1)}, bf16[2,512,256]{2,1,0:T(8,128)(2,1)S(1)}, u32[]{:S(2)}, u32[]{:S(2)}) collective-permute-start(bf16[2,512,256]{2,1,0:T(8,128)(2,1)S(1)} %shard_map.66.refs_1_), channel_id=1, source_target_pairs={{0,1},{1,2},{2,3},{3,4},{4,5},{5,6},{6,7},{7,8},{8,9},{9,10},{10,1... | collective-permute-start | bytes 1572872 | tf_op jit(solution)/shard_map/ppermute | solution.py:19
  13.8 0.0 collective-permute-done.1.refs_0_
  13.8 3.4 %shard_map.67.refs_0_.refs_1_ = bf16[2,512,256]{2,1,0:T(8,128)(2,1)S(1)} custom-call(bf16[2,512,256]{2,1,0:T(8,128)(2,1)S(1)} %collective-permute-done.1.refs_0_, bf16[4,4,128,768]{3,2,1,0:T(8,128)(2,1)S(1)} %shard_map.65.refs_0_.refs_1_, bf16[4,512,256]{2,1,0:T(8,128)(2,1)S(1)} %copy-done, f32[1,256]{1,0:T(1,128)S(1)} %get-tuple-element.7.gain_ref.refs_3_, ...), custom_call_target="tpu_custom_call" | custom-call | flops 3623878656 | bytes 3538944 | tf_op jit(solution)/shard_map/pallas_call | solution.py:192
  17.2 0.0 copy-done.3
  17.2 0.0 copy-done.4
  17.2 0.0 copy-done.5
  17.2 3.6 %shard_map.68.refs_5_ = bf16[16,4,32,256]{3,2,1,0:T(8,128)(2,1)S(1)} custom-call(bf16[2,512,256]{2,1,0:T(8,128)(2,1)S(1)} %shard_map.67.refs_0_.refs_1_, bf16[2,512,256]{2,1,0:T(8,128)(2,1)S(1)} %shard_map.66.refs_1_, f32[1,256]{1,0:T(1,128)S(1)} %bitcast.10, bf16[3,3,768,256]{3,2,1,0:T(8,128)(2,1)S(1)} %bitcast.8, bf16[256,256]{1,0:T(8,128)(2,1)S(1)} %copy-done.4), custom_call_target="tpu_custom_call" | custom-call | flops 3623878656 | bytes 3538944 | tf_op jit(solution)/shard_map/pallas_call | solution.py:192
  20.8 0.0 collective-permute-done.refs_0_
  20.8 3.6 %shard_map.69 = bf16[16,4,32,256]{3,2,1,0:T(8,128)(2,1)S(1)} custom-call(bf16[2,512,256]{2,1,0:T(8,128)(2,1)S(1)} %collective-permute-done.refs_0_, bf16[2,512,256]{2,1,0:T(8,128)(2,1)S(1)} %shard_map.67.refs_0_.refs_1_, f32[1,256]{1,0:T(1,128)S(1)} %bitcast.11, bf16[3,3,768,256]{3,2,1,0:T(8,128)(2,1)S(1)} %bitcast.9, ...), custom_call_target="tpu_custom_call", output_to_operand_aliasing={{}: (5, {})} | custom-call | flops 3623878656 | bytes 3538944 | tf_op jit(solution)/shard_map/pallas_call | solution.py:192
  24.4 31.3 %all_to_all.5 = bf16[16,4,32,256]{3,2,1,0:T(8,128)(2,1)S(1)} all-to-all(bf16[16,4,32,256]{3,2,1,0:T(8,128)(2,1)S(1)} %shard_map.69), channel_id=1, replica_groups=mesh['clip'=2,'tm'=16] {'tm'}, dimensions={0} | all-to-all | bytes 2097152 | tf_op jit(solution)/shard_map/all_to_all | solution.py:228
  55.7 1.0 %copy.10 = bf16[64,32,256]{2,1,0:T(8,128)(2,1)} copy(bf16[64,32,256]{2,1,0:T(8,128)(2,1)S(1)} %bitcast.12) | data formatting | bytes 2097152
  (1 shorter events, 0.0 us)
Async XLA Ops:
  0.0 1.2 %copy-start = (bf16[4,512,256]{2,1,0:T(8,128)(2,1)S(1)}, bf16[4,512,256]{2,1,0:T(8,128)(2,1)}, u32[]{:S(2)}) copy-start(bf16[4,512,256]{2,1,0:T(8,128)(2,1)} %refs_2_.3) | copy-start | bytes 3145732
  1.2 0.7 %copy-start.1 = (f32[256]{0:T(256)S(1)}, f32[256]{0:T(256)}, u32[]{:S(2)}) copy-start(f32[256]{0:T(256)} %param.7) | copy-start | bytes 3076
  1.9 6.4 %copy-start.2 = (bf16[3,3,3,256,256]{4,3,2,1,0:T(8,128)(2,1)S(1)}, bf16[3,3,3,256,256]{4,3,2,1,0:T(8,128)(2,1)}, u32[]{:S(2)}) copy-start(bf16[3,3,3,256,256]{4,3,2,1,0:T(8,128)(2,1)} %param.8) | copy-start | bytes 10616836
  1.9 11.8 %collective-permute-start.1 = (bf16[2,512,256]{2,1,0:T(8,128)(2,1)S(1)}, bf16[2,512,256]{2,1,0:T(8,128)(2,1)S(1)}, u32[]{:S(2)}, u32[]{:S(2)}) collective-permute-start(bf16[2,512,256]{2,1,0:T(8,128)(2,1)S(1)} %get-tuple-element.8), channel_id=1, source_target_pairs={{0,1},{1,2},{2,3},{3,4},{4,5},{5,6},{6,7},{7,8},{8,9},{9,10},{10,1... | collective-permute-start | bytes 1572872 | tf_op jit(solution)/shard_map/ppermute | solution.py:19
  11.5 5.6 %copy-start.3 = (bf16[3,3,3,256,256]{4,3,2,1,0:T(8,128)(2,1)S(1)}, bf16[3,3,3,256,256]{4,3,2,1,0:T(8,128)(2,1)}, u32[]{:S(2)}) copy-start(bf16[3,3,3,256,256]{4,3,2,1,0:T(8,128)(2,1)} %param.10) | copy-start | bytes 10616836
  11.5 5.6 %copy-start.4 = (bf16[256,256]{1,0:T(8,128)(2,1)S(1)}, bf16[256,256]{1,0:T(8,128)(2,1)}, u32[]{:S(2)}) copy-start(bf16[256,256]{1,0:T(8,128)(2,1)} %refs_4_.3) | copy-start | bytes 393220
  11.6 5.6 %copy-start.5 = (f32[256]{0:T(256)S(1)}, f32[256]{0:T(256)}, u32[]{:S(2)}) copy-start(f32[256]{0:T(256)} %param.9) | copy-start | bytes 3076
  11.6 9.2 %collective-permute-start = (bf16[2,512,256]{2,1,0:T(8,128)(2,1)S(1)}, bf16[2,512,256]{2,1,0:T(8,128)(2,1)S(1)}, u32[]{:S(2)}, u32[]{:S(2)}) collective-permute-start(bf16[2,512,256]{2,1,0:T(8,128)(2,1)S(1)} %shard_map.66.refs_1_), channel_id=1, source_target_pairs={{0,1},{1,2},{2,3},{3,4},{4,5},{5,6},{6,7},{7,8},{8,9},{9,10},{10,1... | collective-permute-start | bytes 1572872 | tf_op jit(solution)/shard_map/ppermute | solution.py:19
